TPU v7x, 128 devices: a whole 4x4x4 slice. The times are simulated.
128 devices in a mesh: chan: 4 (over y), tm: 32 (over z, x, core).
Axes of the slice: x: 4, y: 4, z: 4, core: 2. Of those that a mesh axis runs over, the one named last changes fastest.
Arguments:
- strain: float32 [768, 524288], P('chan', 'tm'), may hold values from -6 to 6
Outputs:
- power: float32 [768, 8192], P('chan', 'tm')
- nyquist: float32 [768], P('chan')
- mean_power: float32 [8192], P('tm')
All inputs are finite; a program needn't handle non-finite values.
Results may differ from a plain program's by a relative error of at most 0.00007.
Values sent between devices are 32-bit elements; how exact they have to be, the bound alone decides.
No kernel may reach another device: no remote copies, remote signals or barrier semaphores. Data moves between devices by JAX's collectives and lax.ppermute only.
A program may use at most 192 MiB of HBM per device.

v0:
```python
import jax
import jax.numpy as jnp
from jax import lax
from jax.sharding import PartitionSpec as P

ROOT = 128


highest_mode = lax.Precision.HIGHEST


def shifted(block, axis, distance):
    devices = range(lax.axis_size(axis))
    route = [(i - distance, i) for i in devices if i - distance in devices]
    return lax.ppermute(block, axis, route)


def copy_for_each(array, axis):
    devices = lax.axis_size(axis)
    return lax.all_to_all(
        jnp.broadcast_to(array[None], (devices, *array.shape)), axis, 0, 0, tiled=True
    )


def over_copies(array, axis):
    everything = copy_for_each(array, axis)
    return jnp.sum(everything, axis=0)


def hann_window(seg_len):
    sample_pos = jnp.arange(seg_len, dtype=jnp.float32)
    return 0.5 - 0.5 * jnp.cos(2.0 * jnp.pi * sample_pos / seg_len)


def dft_tables(root_len):
    positions = jnp.arange(root_len, dtype=jnp.int32)
    products = positions[:, None] * positions[None, :]
    short_angle = 2.0 * jnp.pi * (products % root_len).astype(jnp.float32) / root_len
    long_angle = 2.0 * jnp.pi * products.astype(jnp.float32) / (root_len * root_len)
    half_root = root_len // 2
    parity = (1 - 2 * (positions % 2)).astype(jnp.float32)
    return (
        jnp.cos(short_angle),
        jnp.sin(short_angle),
        jnp.cos(long_angle),
        jnp.sin(long_angle),
        jnp.cos(short_angle[:half_root]),
        jnp.sin(short_angle[:half_root]),
        parity,
    )


def periodogram(pieces, tables, window):
    cos_short, sin_short, cos_long, sin_long, cos_half, sin_half, parity = tables
    root_len = cos_short.shape[0]
    piece_rows = pieces.shape[0]
    centred = (pieces - jnp.mean(pieces, axis=1, keepdims=True)) * window
    folded = centred.reshape(piece_rows, root_len, root_len)
    real_first = jnp.einsum("ka,rab->rkb", cos_short, folded, precision=highest_mode)
    imag_first = -jnp.einsum("ka,rab->rkb", sin_short, folded, precision=highest_mode)
    real_twist = real_first * cos_long + imag_first * sin_long
    imag_twist = imag_first * cos_long - real_first * sin_long
    real_final = jnp.einsum(
        "rkb,qb->rqk", real_twist, cos_half, precision=highest_mode
    ) + jnp.einsum("rkb,qb->rqk", imag_twist, sin_half, precision=highest_mode)
    imag_final = jnp.einsum(
        "rkb,qb->rqk", imag_twist, cos_half, precision=highest_mode
    ) - jnp.einsum("rkb,qb->rqk", real_twist, sin_half, precision=highest_mode)
    spectrum_power = (real_final * real_final + imag_final * imag_final).reshape(piece_rows, -1)
    edge_term = jnp.sum(folded * parity, axis=(1, 2))
    return (spectrum_power, edge_term * edge_term)


def per_device(strain):
    chan_rows, time_width = strain.shape
    seg_len = ROOT * ROOT
    half_len = seg_len // 2
    window = hann_window(seg_len)
    energy = jnp.sum(window * window)
    tables = dft_tables(ROOT)
    tm_count = lax.axis_size("tm")
    block_count = time_width // half_len
    segments = block_count * tm_count - 1
    band_width = half_len // tm_count
    follower = shifted(strain[:, :half_len], "tm", -1)
    extended = jnp.concatenate([strain, follower], axis=1)
    is_last = (lax.axis_index("tm") == tm_count - 1).astype(jnp.float32)
    running_total = jnp.zeros((chan_rows, half_len), jnp.float32)
    nyquist_part = jnp.zeros((chan_rows,), jnp.float32)
    for segment_index in range(block_count):
        start = segment_index * half_len
        spectrum_power, edge_term = periodogram(
            extended[:, start : start + seg_len], tables, window
        )
        if segment_index == block_count - 1:
            keep_factor = 1.0 - is_last
            spectrum_power = spectrum_power * keep_factor
            edge_term = edge_term * keep_factor
        running_total = running_total + spectrum_power
        nyquist_part = nyquist_part + edge_term
    band_total = lax.psum_scatter(running_total, "tm", scatter_dimension=1, tiled=True)
    edges_total = over_copies(nyquist_part, "tm")
    bin_index = lax.axis_index("tm") * band_width + jnp.arange(band_width, dtype=jnp.int32)
    doubling = jnp.where(bin_index == 0, 1.0, 2.0).astype(jnp.float32)
    power = band_total * doubling / (segments * energy)
    nyquist = edges_total / (segments * energy)
    channel_sum = over_copies(jnp.sum(power, axis=0), "chan")
    mean_power = channel_sum / (chan_rows * lax.axis_size("chan"))
    return (power, nyquist, mean_power)


def solution(mesh):
    in_specs = (P("chan", "tm"),)
    out_specs = (P("chan", "tm"), P("chan"), P("tm"))
    return jax.shard_map(
        per_device, mesh=mesh, in_specs=in_specs, out_specs=out_specs, check_vma=False
    )
```

profile of v0, /device:TPU:0, one launch (start us, length us, event | category | flops | bytes accessed | tf_op | source)
XLA Modules:
  0.0 477.9 jit_solution(821330667707972011)
XLA Ops:
  7.2 6.1 %slice.25 = f32[192,8192]{1,0:T(8,128)} slice(f32[192,16384]{1,0:T(8,128)} %param.1), slice={[0:192], [0:8192]} | slice | bytes 12582912 | tf_op jit(solution)/shard_map/slice | solution.py:85
  15.6 10.1 %collective-permute-done = f32[192,8192]{1,0:T(8,128)} collective-permute-done((f32[192,8192]{1,0:T(8,128)}, f32[192,8192]{1,0:T(8,128)}, u32[]{:S(2)}, u32[]{:S(2)}) %collective-permute-start) | collective-permute-done | bytes 6291488 | tf_op jit(solution)/shard_map/ppermute | solution.py:15
  25.6 9.8 %fusion.74 = (f32[192]{0:T(256)S(1)}, f32[192]{0:T(256)S(1)}) fusion(f32[192,16384]{1,0:T(8,128)} %param.1, f32[192,8192]{1,0:T(8,128)} %collective-permute-done), kind=kLoop, calls=%fused_computation.93 | loop fusion | flops 9436800 | bytes 18875904 | tf_op jit(solution)/shard_map/reduce_sum | solution.py:57
  35.5 22.8 %multiply_reduce_fusion.1 = (f32[192]{0:T(256)S(1)}, f32[192]{0:T(256)S(1)}, f32[24,8,128,128]{3,1,2,0:T(8,128)}, f32[24,8,128,128]{3,1,2,0:T(8,128)}) fusion(f32[192,16384]{1,0:T(8,128)} %param.1, f32[16384]{0:T(1024)S(1)} %broadcast_bitcast_fusion, f32[16384]{0:T(1024)S(1)} %multiply_subtract_fusion, f32[192]{0:T(256)S(1)} %get-tuple-element.12, ...), kind=kLoop, calls=%fused_computation.14 | loop fusion | flops 28311168 | bytes 44174336 | tf_op jit(solution)/shard_map/reduce_sum | solution.py:70
  58.3 11.5 %copy.62 = f32[24,8,128,128]{3,2,1,0:T(8,128)} copy(f32[24,8,128,128]{3,1,2,0:T(8,128)} %get-tuple-element.10) | data formatting | bytes 25165824
  69.8 24.5 %fusion.30 = f32[192,128,128]{2,1,0:T(8,128)S(1)} fusion(f32[192,128,128]{2,1,0:T(8,128)} %bitcast.93), kind=kOutput, calls=%fused_computation.39 | convolution fusion | flops 4832067584 | bytes 25165824 | tf_op jit(solution)/shard_map/ka,rab->rkb/dot_general | solution.py:60
  94.4 23.6 %fusion.34 = f32[192,128,128]{2,1,0:T(8,128)} fusion(f32[192,128,128]{2,1,0:T(8,128)S(1)} %bitcast.96), kind=kOutput, calls=%fused_computation.43 | convolution fusion | flops 4832067584 | bytes 25165824 | tf_op jit(solution)/shard_map/ka,rab->rkb/dot_general | solution.py:59
  117.9 13.1 %fusion.10 = f32[64,192,128]{2,0,1:T(8,128)} fusion(f32[192,128,128]{2,1,0:T(8,128)} %fusion.34, f32[192,128,128]{2,1,0:T(8,128)S(1)} %fusion.30, f32[128,128]{0,1:T(8,128)S(1)} %copy.35, f32[128,128]{0,1:T(8,128)S(1)} %copy.33, f32[128,128]{1,0:T(8,128)S(1)} %fusion.27), kind=kOutput, calls=%fused_computation.23 | convolution fusion | flops 2428502016 | bytes 31621120 | tf_op jit(solution)/shard_map/rkb,qb->rqk/dot_general | solution.py:68
  131.1 13.2 %fusion.12 = f32[64,192,128]{2,0,1:T(8,128)} fusion(f32[192,128,128]{2,1,0:T(8,128)} %fusion.34, f32[192,128,128]{2,1,0:T(8,128)S(1)} %fusion.30, f32[128,128]{0,1:T(8,128)S(1)} %copy.35, f32[128,128]{0,1:T(8,128)S(1)} %copy.33, f32[128,128]{1,0:T(8,128)S(1)} %fusion.27), kind=kOutput, calls=%fused_computation.24 | convolution fusion | flops 2428502016 | bytes 31621120 | tf_op jit(solution)/shard_map/rkb,qb->rqk/dot_general | solution.py:63
  144.3 12.9 %fusion.6 = f32[64,192,128]{2,0,1:T(8,128)} fusion(f32[192,128,128]{2,1,0:T(8,128)} %fusion.34, f32[192,128,128]{2,1,0:T(8,128)S(1)} %fusion.30, f32[128,128]{0,1:T(8,128)S(1)} %copy.35, f32[128,128]{0,1:T(8,128)S(1)} %copy.33, f32[128,128]{1,0:T(8,128)S(1)} %fusion.27), kind=kOutput, calls=%fused_computation.21 | convolution fusion | flops 2428502016 | bytes 31621120 | tf_op jit(solution)/shard_map/rkb,qb->rqk/dot_general | solution.py:66
  157.3 12.9 %fusion.8 = f32[64,192,128]{2,0,1:T(8,128)} fusion(f32[192,128,128]{2,1,0:T(8,128)} %fusion.34, f32[192,128,128]{2,1,0:T(8,128)S(1)} %fusion.30, f32[128,128]{0,1:T(8,128)S(1)} %copy.35, f32[128,128]{0,1:T(8,128)S(1)} %copy.33, f32[128,128]{1,0:T(8,128)S(1)} %fusion.27), kind=kOutput, calls=%fused_computation.22 | convolution fusion | flops 2428502016 | bytes 31621120 | tf_op jit(solution)/shard_map/rkb,qb->rqk/dot_general | solution.py:65
  170.1 11.4 %copy.63 = f32[24,8,128,128]{3,2,1,0:T(8,128)} copy(f32[24,8,128,128]{3,1,2,0:T(8,128)} %get-tuple-element.9) | data formatting | bytes 25165824
  181.5 24.7 %fusion.28 = f32[192,128,128]{2,1,0:T(8,128)S(1)} fusion(f32[192,128,128]{2,1,0:T(8,128)} %bitcast.97), kind=kOutput, calls=%fused_computation.37 | convolution fusion | flops 4832067584 | bytes 25165824 | tf_op jit(solution)/shard_map/ka,rab->rkb/dot_general | solution.py:60
  206.3 23.5 %fusion.32 = f32[192,128,128]{2,1,0:T(8,128)} fusion(f32[192,128,128]{2,1,0:T(8,128)S(1)} %bitcast.100), kind=kOutput, calls=%fused_computation.41 | convolution fusion | flops 4832067584 | bytes 25165824 | tf_op jit(solution)/shard_map/ka,rab->rkb/dot_general | solution.py:59
  229.8 12.8 %fusion.16 = f32[64,192,128]{2,0,1:T(8,128)} fusion(f32[192,128,128]{2,1,0:T(8,128)} %fusion.32, f32[192,128,128]{2,1,0:T(8,128)S(1)} %fusion.28, f32[128,128]{0,1:T(8,128)S(1)} %copy.35, f32[128,128]{0,1:T(8,128)S(1)} %copy.33, f32[128,128]{1,0:T(8,128)S(1)} %fusion.27), kind=kOutput, calls=%fused_computation.26 | convolution fusion | flops 2428502016 | bytes 31621120 | tf_op jit(solution)/shard_map/rkb,qb->rqk/dot_general | solution.py:65
  242.6 13.3 %fusion.18 = f32[64,192,128]{2,0,1:T(8,128)} fusion(f32[192,128,128]{2,1,0:T(8,128)} %fusion.32, f32[192,128,128]{2,1,0:T(8,128)S(1)} %fusion.28, f32[128,128]{0,1:T(8,128)S(1)} %copy.35, f32[128,128]{0,1:T(8,128)S(1)} %copy.33, f32[128,128]{1,0:T(8,128)S(1)} %fusion.27), kind=kOutput, calls=%fused_computation.27 | convolution fusion | flops 2428502016 | bytes 31621120 | tf_op jit(solution)/shard_map/rkb,qb->rqk/dot_general | solution.py:68
  255.9 12.9 %fusion.14 = f32[64,192,128]{2,0,1:T(8,128)} fusion(f32[192,128,128]{2,1,0:T(8,128)} %fusion.32, f32[192,128,128]{2,1,0:T(8,128)S(1)} %fusion.28, f32[128,128]{0,1:T(8,128)S(1)} %copy.35, f32[128,128]{0,1:T(8,128)S(1)} %copy.33, f32[128,128]{1,0:T(8,128)S(1)} %fusion.27), kind=kOutput, calls=%fused_computation.25 | convolution fusion | flops 2428502016 | bytes 31621120 | tf_op jit(solution)/shard_map/rkb,qb->rqk/dot_general | solution.py:66
  268.8 28.2 %multiply_add_fusion = f32[64,192,128]{2,0,1:T(8,128)} fusion(f32[64,192,128]{2,0,1:T(8,128)} %fusion.14, f32[64,192,128]{2,0,1:T(8,128)} %fusion.18, f32[64,192,128]{2,0,1:T(8,128)} %fusion.16, f32[64,192,128]{2,0,1:T(8,128)} %fusion.6, f32[64,192,128]{2,0,1:T(8,128)} %fusion.10, f32[64,192,128]{2,0,1:T(8,128)} %fusion.12, f32[64,192,128]{2,0,1:T(8,128)} %fusion.8, ...), kind=kOutput, calls=%fused_computation.20 | convolution fusion | flops 2447376384 | bytes 75661312 | tf_op jit(solution)/shard_map/rkb,qb->rqk/dot_general | solution.py:63
  297.0 10.9 %copy.66 = f32[24,8,64,128]{3,1,2,0:T(8,128)} copy(f32[24,8,64,128]{3,2,1,0:T(8,128)} %bitcast.102) | data formatting | bytes 12582912
  308.6 69.6 %all-to-all-start = ((f32[32,1,192]{2,1,0:T(1,128)}), f32[32,1,192]{2,1,0:T(1,128)S(1)}, u32[]{:S(2)}, u32[]{:S(2)}) async-start(f32[32,1,192]{2,1,0:T(1,128)} %broadcast_in_dim.12), calls=%async_computation.1 | async-start | bytes 65536 | tf_op jit(solution)/shard_map/all_to_all | solution.py:20
  379.8 5.9 %all-to-all-done = f32[32,1,192]{2,1,0:T(1,128)S(1)} async-done(((f32[32,1,192]{2,1,0:T(1,128)}), f32[32,1,192]{2,1,0:T(1,128)S(1)}, u32[]{:S(2)}, u32[]{:S(2)}) %all-to-all-start) | async-done | bytes 24608 | tf_op jit(solution)/shard_map/all_to_all | solution.py:20
  385.7 72.6 %reduce-scatter.2.cloned.1.call-done = f32[192,256]{1,0:T(8,128)} async-done(((f32[192,8192]{1,0:T(8,128)}), f32[192,256]{1,0:T(8,128)}) %reduce-scatter.2.cloned.1.call-update) | async-done | bytes 196624 | tf_op jit(solution)/shard_map/reduce_scatter | solution.py:101
  460.6 4.3 all-to-all-start.1
  465.5 4.7 all-to-all-done.1
  (38 shorter events, 7.2 us)
Async XLA Ops:
  7.2 451.2 %reduce-scatter.2.cloned.1.call-start = ((), (), s32[]{:S(2)}) async-start(), calls=%async_computation.3 | async-start | bytes 6488064 | tf_op jit(solution)/shard_map/reduce_scatter | solution.py:101
  13.3 12.4 %collective-permute-start = (f32[192,8192]{1,0:T(8,128)}, f32[192,8192]{1,0:T(8,128)}, u32[]{:S(2)}, u32[]{:S(2)}) collective-permute-start(f32[192,8192]{1,0:T(8,128)} %slice.25), channel_id=1, source_target_pairs={{1,0},{2,1},{3,2},{4,3},{5,4},{6,5},{7,6},{8,7},{9,8},{10,9},{11,1... | collective-permute-start | bytes 18874376 | tf_op jit(solution)/shard_map/ppermute | solution.py:15
  69.8 24.5 %slice-start = ((s8[12582912]{0:T(1024)(128)(4,1)}), s8[4194304]{0:T(1024)(128)(4,1)S(1)}, s32[]{:S(2)}) async-start(s8[12582912]{0:T(1024)(128)(4,1)} %bitcast.94), calls=%async_computation.4 | async-start | bytes 8388608
  69.8 24.5 %slice-start.1 = ((s8[12582912]{0:T(1024)(128)(4,1)}), s8[4194304]{0:T(1024)(128)(4,1)S(1)}, s32[]{:S(2)}) async-start(s8[12582912]{0:T(1024)(128)(4,1)} %bitcast.94), calls=%async_computation.5 | async-start | bytes 8388608
  69.8 24.6 %slice-start.2 = ((s8[12582912]{0:T(1024)(128)(4,1)}), s8[4194304]{0:T(1024)(128)(4,1)S(1)}, s32[]{:S(2)}) async-start(s8[12582912]{0:T(1024)(128)(4,1)} %bitcast.94), calls=%async_computation.6 | async-start | bytes 8388608
  181.5 24.7 %slice-start.3 = ((s8[12582912]{0:T(1024)(128)(4,1)}), s8[4194304]{0:T(1024)(128)(4,1)S(1)}, s32[]{:S(2)}) async-start(s8[12582912]{0:T(1024)(128)(4,1)} %bitcast.98), calls=%async_computation.7 | async-start | bytes 8388608
  181.5 24.7 %slice-start.4 = ((s8[12582912]{0:T(1024)(128)(4,1)}), s8[4194304]{0:T(1024)(128)(4,1)S(1)}, s32[]{:S(2)}) async-start(s8[12582912]{0:T(1024)(128)(4,1)} %bitcast.98), calls=%async_computation.8 | async-start | bytes 8388608
  181.5 24.7 %slice-start.5 = ((s8[12582912]{0:T(1024)(128)(4,1)}), s8[4194304]{0:T(1024)(128)(4,1)S(1)}, s32[]{:S(2)}) async-start(s8[12582912]{0:T(1024)(128)(4,1)} %bitcast.98), calls=%async_computation.9 | async-start | bytes 8388608
  206.2 49.6 %copy-start = (f32[192,128,128]{2,1,0:T(8,128)}, f32[192,128,128]{2,1,0:T(8,128)S(1)}, u32[]{:S(2)}) copy-start(f32[192,128,128]{2,1,0:T(8,128)S(1)} %fusion.28) | copy-start | bytes 37748740
  308.6 77.0 %all-to-all-start = ((f32[32,1,192]{2,1,0:T(1,128)}), f32[32,1,192]{2,1,0:T(1,128)S(1)}, u32[]{:S(2)}, u32[]{:S(2)}) async-start(f32[32,1,192]{2,1,0:T(1,128)} %broadcast_in_dim.12), calls=%async_computation.1 | async-start | bytes 65536 | tf_op jit(solution)/shard_map/all_to_all | solution.py:20
  460.6 9.6 %all-to-all-start.1 = ((f32[4,1,256]{2,1,0:T(1,128)}), f32[4,1,256]{2,1,0:T(1,128)S(1)}, u32[]{:S(2)}, u32[]{:S(2)}) async-start(f32[4,1,256]{2,1,0:T(1,128)} %broadcast_in_dim.13), calls=%async_computation.2 | async-start | bytes 8192 | tf_op jit(solution)/shard_map/all_to_all | solution.py:20
Sparse Core Ops, SparseCore 0:
  308.1 150.2 reduce-scatter.1
where the time goes:
time: 485 us; the launch traced here: 478 us
  matrix products  216 us (45%)
  waiting for transfers between devices  93.4 us (19%)
  starting transfers between devices  75.2 us (16%)
  local copies, waits for them, and re-layouts  41.3 us (9%)
  other arithmetic  37.1 us (8%)
  between operations  15.2 us (3%)
    all_to_all x2, starting transfers between devices, copy_for_each(): lax.all_to_all(jnp.broadcast_to(array[None], (devices, *array.shape)), ax...  73.9 us
    reduce_scatter x1, waiting for transfers between devices, per_device(): lax.psum_scatter(running_total, 'tm', scatter_dimension=1, tiled=True)  72.6 us
    dot_general x2, matrix products, periodogram(): jnp.einsum('ka,rab->rkb', sin_short, folded, precision=highest_mode)  49.2 us
    dot_general x2, matrix products, periodogram(): jnp.einsum('ka,rab->rkb', cos_short, folded, precision=highest_mode)  47.1 us
    dot_general x2, matrix products, periodogram(): jnp.einsum('rkb,qb->rqk', real_twist, cos_half, precision=highest_mode)  41.5 us
    unnamed x17, local copies, waits for them, and re-layouts  33.8 us
    dot_general x2, matrix products, periodogram(): jnp.einsum('rkb,qb->rqk', real_twist, sin_half, precision=highest_mode)  26.4 us
    dot_general x2, matrix products, periodogram(): jnp.einsum('rkb,qb->rqk', imag_twist, cos_half, precision=highest_mode)  25.8 us
  transfers between devices with their start and end apart: 4, of which 4 were waited for; matrix products, arithmetic and copies ran while one was open for 1% of the time, Pallas kernels for 0%

commit v1 on v0

v1 whole, which is shorter than its diff:
```python
import functools

import jax
import jax.numpy as jnp
import numpy as np
from jax import lax
from jax.experimental import pallas as pl
from jax.experimental.pallas import tpu as pltpu
from jax.sharding import PartitionSpec as P

SEG = 16384
ROOT = 128
HALF = ROOT // 2
TILE = 8
LANES = 128
STEPS = 4


def split_bf16(table):
    high = table.astype(jnp.bfloat16)
    low = (table - high.astype(np.float64)).astype(jnp.bfloat16)
    return high, low


def dft_constants():
    n = np.arange(ROOT)
    angle = 2.0 * np.pi * ((n[:, None] * n[None, :]) % ROOT) / ROOT
    rows = np.arange(HALF)
    first = np.concatenate([np.cos(angle[:HALF]), -np.sin(angle[:HALF])], axis=0)
    first[HALF] = 1.0 - 2.0 * (n % 2)
    high, low = split_bf16(first)
    first_high = np.concatenate([high, high], axis=1)
    twist = 2.0 * np.pi * (rows[:, None] * n[None, :]) / SEG
    cos_twist = np.cos(twist)
    cos_imag = cos_twist.copy()
    cos_imag[0] = 0.0
    twiddle = np.stack([cos_twist, cos_imag, np.sin(twist)]).astype(np.float32)
    edge = np.pi * n / ROOT
    edge_twiddle = np.stack([np.cos(edge), -np.sin(edge)]).astype(np.float32)
    halves = []
    for core in range(2):
        columns = []
        for half in (core, 1 - core):
            for place in range(16):
                shard = 2 * place + half
                for k in (2 * shard, 2 * shard + 1):
                    columns += [k, ROOT - 1 - k]
        halves.append(columns)
    second = []
    for columns in halves:
        c = np.cos(angle[:, columns])
        s = np.sin(angle[:, columns])
        full = np.block([[c, -s], [s, c]])
        h, l = split_bf16(full)
        second.append(np.concatenate([h, h, l], axis=0))
    return first_high, low, twiddle, edge_twiddle, np.stack(second)


def window_tables():
    pos = jnp.arange(SEG, dtype=jnp.float32)
    window = 0.5 - 0.5 * jnp.cos(2.0 * jnp.pi * pos / SEG)
    energy = jnp.sum(window * window)
    plain = window.reshape(ROOT, LANES)
    swapped = jnp.concatenate([plain[HALF:], plain[:HALF]], axis=0)
    return jnp.stack([plain, swapped]), energy


def spectrum_kernel(
    tiles,
    step,
    meta,
    x_ref,
    left_ref,
    right_ref,
    plain_ref,
    window_ref,
    first_ref,
    first_low_ref,
    twiddle_ref,
    edge_ref,
    second_ref,
    edges_in_ref,
    own_ref,
    other_ref,
    edges_ref,
    halo,
    spec,
    corner,
    result,
):
    i = pl.program_id(0)
    is_right = i >= tiles
    core = meta[0]

    @pl.when(i < tiles)
    def _():
        halo[...] = left_ref[0]

    @pl.when(is_right)
    def _():
        halo[...] = right_ref[0]

    @pl.when(i == 0)
    def _():
        edges_ref[...] = edges_in_ref[...]

    own_start = jnp.where(is_right, 0, HALF * TILE)
    keep = jnp.where(is_right, meta[2], meta[1]).astype(jnp.float32)
    cos_real = twiddle_ref[0]
    cos_imag = twiddle_ref[1]
    sin_both = twiddle_ref[2]
    for pair in range(TILE // 2):
        for seg in range(2):
            highs = []
            lows = []
            for c in (2 * pair, 2 * pair + 1):
                if seg == 0:
                    piece = x_ref[0, pl.ds(c, ROOT, stride=TILE), :]
                    window = plain_ref[0]
                else:
                    own = x_ref[0, pl.ds(own_start + c, HALF, stride=TILE), :]
                    piece = jnp.concatenate([own, halo[pl.ds(c, HALF, stride=TILE), :]], axis=0)
                    window = window_ref[0]
                mean = jnp.sum(piece, keepdims=True) * (1.0 / SEG)
                centred = (piece - mean) * window
                high = centred.astype(jnp.bfloat16)
                highs.append(high)
                lows.append((centred - high.astype(jnp.float32)).astype(jnp.bfloat16))
            high = jnp.concatenate(highs, axis=1)
            low = jnp.concatenate(lows, axis=1)
            stage = jnp.dot(
                first_ref[...], jnp.concatenate([high, low], axis=0), preferred_element_type=jnp.float32
            ) + jnp.dot(first_low_ref[...], high, preferred_element_type=jnp.float32)
            for q in range(2):
                c = 2 * pair + q
                real = stage[:HALF, q * LANES : (q + 1) * LANES]
                imag = stage[HALF:, q * LANES : (q + 1) * LANES]
                corner[seg * TILE + c : seg * TILE + c + 1, :] = imag[0:1]
                row = (seg * TILE + c) * HALF
                turned = (real * cos_real + imag * sin_both, imag * cos_imag - real * sin_both)
                for part in range(2):
                    value = turned[part]
                    high = value.astype(jnp.bfloat16)
                    lanes = slice(part * LANES, (part + 1) * LANES)
                    lanes_low = slice((2 + part) * LANES, (3 + part) * LANES)
                    spec[row : row + HALF, lanes] = high
                    spec[row : row + HALF, lanes_low] = (value - high.astype(jnp.float32)).astype(jnp.bfloat16)
    rows = 2 * TILE * HALF
    for part in range(2):
        value = corner[...] * edge_ref[part : part + 1]
        high = value.astype(jnp.bfloat16)
        spec[rows : rows + 2 * TILE, part * LANES : (part + 1) * LANES] = high
        spec[rows : rows + 2 * TILE, (2 + part) * LANES : (3 + part) * LANES] = (
            value - high.astype(jnp.float32)
        ).astype(jnp.bfloat16)
    weight = second_ref[0]
    result[...] = jnp.dot(spec[...], weight[: 4 * LANES], preferred_element_type=jnp.float32) + jnp.dot(
        spec[:, : 2 * LANES], weight[4 * LANES :], preferred_element_type=jnp.float32
    )

    def power_of(start, size):
        real = result[start : start + size, :LANES]
        imag = result[start : start + size, LANES:]
        return real * real + imag * imag

    edge_power = power_of(rows, TILE) + keep * power_of(rows + TILE, TILE)
    row_id = lax.broadcasted_iota(jnp.int32, (HALF, LANES), 0)
    lane_id = lax.broadcasted_iota(jnp.int32, (HALF, LANES), 1)
    replaced = (row_id == 0) & (lane_id % 2 == 1)
    tile_lane = lax.broadcasted_iota(jnp.int32, (TILE, LANES), 1)
    tile_row = lax.broadcasted_iota(jnp.int32, (TILE, LANES), 0)
    edge_lane = HALF - 1 + HALF * (1 - core)
    edge_tile = jnp.zeros((TILE, LANES), jnp.float32)
    columns = []
    for pair in range(TILE // 2):
        blocks = []
        for q in range(2):
            c = 2 * pair + q
            total = power_of(c * HALF, HALF) + keep * power_of((TILE + c) * HALF, HALF)
            edge_tile = jnp.where(tile_row == c, total[0:1], edge_tile)
            blocks.append(jnp.where(replaced, edge_power[c : c + 1], total))
        columns.append(jnp.concatenate(blocks, axis=0).T)
    edge_value = jnp.sum(jnp.where(tile_lane == edge_lane, edge_tile, 0.0), axis=1, keepdims=True)
    tile_number = jnp.where(is_right, 12 + i - tiles, i) + tiles * step
    edges_ref[...] = jnp.where(tile_lane == tile_number, edge_value, edges_ref[...])
    lower = tile_row < 4
    for group in range(2):
        a, b = columns[2 * group], columns[2 * group + 1]
        for half in range(2):
            out = own_ref if half == 0 else other_ref
            for place in range(8):
                start = half * HALF + place * TILE
                va, vb = a[start : start + TILE], b[start : start + TILE]
                out[2 * place, group] = jnp.where(lower, va, pltpu.roll(vb, 4, 0))
                out[2 * place + 1, group] = jnp.where(lower, pltpu.roll(va, 4, 0), vb)


def spectrum(step, tiles, meta, x, left, right, windows, constants, edges):
    first_high, first_low, twiddle, edge_twiddle, second = constants
    groups = 4 * tiles

    def tile_of(i):
        return jnp.where(i >= tiles, 12 + i - tiles, i) + tiles * step

    whole = lambda shape: pl.BlockSpec(shape, lambda i, m: (0,) * len(shape))
    out_block = pl.BlockSpec((16, 2, TILE, LANES), lambda i, m: (0, i, 0, 0))
    out_type = jax.ShapeDtypeStruct((16, groups, TILE, LANES), jnp.float32)
    return pl.pallas_call(
        functools.partial(spectrum_kernel, tiles, step),
        grid_spec=pltpu.PrefetchScalarGridSpec(
            num_scalar_prefetch=1,
            grid=(2 * tiles,),
            in_specs=[
                pl.BlockSpec((1, ROOT * TILE, LANES), lambda i, m: (tile_of(i), 0, 0)),
                pl.BlockSpec((1, HALF * TILE, LANES), lambda i, m: (jnp.minimum(i, tiles - 1), 0, 0)),
                pl.BlockSpec((1, HALF * TILE, LANES), lambda i, m: (jnp.maximum(i - tiles, 0), 0, 0)),
                pl.BlockSpec((1, ROOT, LANES), lambda i, m: (0, 0, 0)),
                pl.BlockSpec((1, ROOT, LANES), lambda i, m: (jnp.where(i >= tiles, 1, 0), 0, 0)),
                whole((ROOT, 2 * LANES)),
                whole((ROOT, LANES)),
                whole((3, HALF, LANES)),
                whole((2, LANES)),
                pl.BlockSpec((1, 6 * LANES, 2 * LANES), lambda i, m: (m[0], 0, 0)),
                whole((TILE, LANES)),
            ],
            out_specs=[out_block, out_block, whole((TILE, LANES))],
            scratch_shapes=[
                pltpu.VMEM((HALF * TILE, LANES), jnp.float32),
                pltpu.VMEM((2 * TILE * (HALF + 1), 4 * LANES), jnp.bfloat16),
                pltpu.VMEM((2 * TILE, LANES), jnp.float32),
                pltpu.VMEM((2 * TILE * (HALF + 1), 2 * LANES), jnp.float32),
            ],
        ),
        out_shape=[out_type, out_type, jax.ShapeDtypeStruct((TILE, LANES), jnp.float32)],
        compiler_params=pltpu.CompilerParams(dimension_semantics=("arbitrary",)),
        name="spectrum",
    )(meta, x, left, right, windows, windows, first_high, first_low, twiddle, edge_twiddle, second, edges)


def pick_constant():
    table = np.zeros((2, 2 * LANES, LANES), np.float32)
    for q in range(2):
        for k in range(HALF):
            table[q, q * HALF + k, k] = 1.0
            table[q, LANES + q * HALF + k, ROOT - k if k else HALF] = 1.0
    return table


def finish_kernel(tiles, meta, scale_ref, pick_ref, edges_ref, *refs):
    parts, (power_ref, mean_ref, nyquist_ref, band, spread) = refs[:STEPS], refs[STEPS:]
    shard = meta[3]
    for step, part in enumerate(parts):
        for side in range(2):
            total = part[0, side * 2 * tiles : (side + 1) * 2 * tiles]
            for source in range(1, 16):
                total = total + part[source, side * 2 * tiles : (side + 1) * 2 * tiles]
            first = (side * 12 + tiles * step) * 2 * TILE
            band[first : first + 2 * tiles * TILE] = total.reshape(2 * tiles * TILE, LANES)
    scale = scale_ref[0]
    lane = lax.broadcasted_iota(jnp.int32, (1, LANES), 1)
    sums = []
    for k in range(2):
        count = band.shape[0] // 4
        lo = band[pl.ds(2 * k, count, stride=4), :]
        hi = band[pl.ds(2 * k + 1, count, stride=4), :]
        both = jnp.concatenate([lo, hi], axis=1)
        first = (lane == 0) & (shard == 0) & (k == 0)
        factor = jnp.where(first, scale, 2.0 * scale)
        total = jnp.zeros((1, LANES), jnp.float32)
        for q in range(2):
            value = (
                jnp.dot(both, pick_ref[q], preferred_element_type=jnp.float32, precision=lax.Precision.HIGHEST)
                * factor
            )
            spread[k, pl.ds(q, count, stride=2), :] = value
            total = total + jnp.sum(value, axis=0, keepdims=True)
        power_ref[:, k * LANES : (k + 1) * LANES] = spread[k]
        sums.append(total)
    mean_ref[...] = jnp.concatenate(sums, axis=1)
    total = edges_ref[0]
    for source in range(1, 16):
        total = total + edges_ref[source]
    nyquist_ref[...] = (total * scale).T[:24]


def finish(tiles, meta, scale, parts, edges, rows):
    vmem = pl.BlockSpec(memory_space=pltpu.VMEM)
    smem = pl.BlockSpec(memory_space=pltpu.SMEM)
    return pl.pallas_call(
        functools.partial(finish_kernel, tiles),
        in_specs=[smem, smem, vmem, vmem] + [vmem] * len(parts),
        out_specs=[vmem, vmem, vmem],
        out_shape=[
            jax.ShapeDtypeStruct((rows, 2 * LANES), jnp.float32),
            jax.ShapeDtypeStruct((1, 2 * LANES), jnp.float32),
            jax.ShapeDtypeStruct((24, TILE), jnp.float32),
        ],
        scratch_shapes=[
            pltpu.VMEM((rows * 2, LANES), jnp.float32),
            pltpu.VMEM((2, rows, LANES), jnp.float32),
        ],
        name="finish",
    )(meta, scale, pick_constant(), edges, *parts)


def per_device(strain):
    rows, width = strain.shape
    count = lax.axis_size("tm")
    me = lax.axis_index("tm")
    row_tiles = rows // TILE
    tiles = row_tiles // 2 // STEPS
    segments = width // (SEG // 2) * count - 1
    x = strain.reshape(row_tiles, TILE, ROOT, LANES).swapaxes(1, 2).reshape(row_tiles, ROOT * TILE, LANES)
    to_left = [(i + 1, i) for i in range(count - 1)]
    to_right = [(i, i + 1) for i in range(count - 1)]
    halos = []
    for step in range(STEPS):
        first = step * tiles
        left = lax.ppermute(x[first : first + tiles, : HALF * TILE], "tm", to_left)
        right = lax.ppermute(x[12 + first : 12 + first + tiles, HALF * TILE :], "tm", to_right)
        halos.append((left, right))
    windows, energy = window_tables()
    scale = (1.0 / (segments * energy)).reshape(1)
    core = me % 2
    meta = jnp.stack([core, (me < count - 1).astype(jnp.int32), (me > 0).astype(jnp.int32), me]).astype(jnp.int32)
    constants = dft_constants()
    swap = [(i, i ^ 1) for i in range(count)]
    places = [[2 * p + c for p in range(count // 2)] for c in range(2)]
    edges = jnp.zeros((TILE, LANES), jnp.float32)
    parts = []
    for step in range(STEPS):
        own, other, edges = spectrum(step, tiles, meta, x, *halos[step], windows, constants, edges)
        if step == STEPS - 1:
            wide = (16, 1, TILE, LANES)
            own = jnp.concatenate([own, jnp.broadcast_to(edges, wide)], axis=1)
            other = jnp.concatenate([other, jnp.broadcast_to(edges, wide)], axis=1)
        mine = own + lax.ppermute(other, "tm", swap)
        parts.append(lax.all_to_all(mine, "tm", 0, 0, axis_index_groups=places, tiled=True))
    all_edges = parts[-1][:, 4 * tiles]
    power, band_sum, nyquist = finish(tiles, meta, scale, parts, all_edges, rows)
    chans = lax.axis_size("chan")
    total = band_sum
    for shift in range(1, chans):
        total = total + lax.ppermute(band_sum, "chan", [(i, (i + shift) % chans) for i in range(chans)])
    mean_power = (total / (rows * chans)).reshape(-1)
    return power, nyquist.reshape(-1), mean_power


def solution(mesh):
    in_specs = (P("chan", "tm"),)
    out_specs = (P("chan", "tm"), P("chan"), P("tm"))
    return jax.shard_map(per_device, mesh=mesh, in_specs=in_specs, out_specs=out_specs, check_vma=False)
```

time: 485 us -> 175 us (0.36); the launches traced: 478 us -> 174 us
  matrix products: 216 us -> 0 us
  waiting for transfers between devices: 93.4 us -> 37.9 us
  Pallas kernels: 0 us -> 52.3 us
  local copies, waits for them, and re-layouts: 41.3 us -> 9.75 us
  other arithmetic: 37.1 us -> 13.7 us
  starting transfers between devices: 75.2 us -> 58.8 us
  between operations: 15.2 us -> 1.55 us
    dot_general x12 -> x0, matrix products: 216 us -> none  [the longest x2 49.2 us: periodogram(): jnp.einsum('ka,rab->rkb', sin_short, folded, precision=highest_mode)]
    reduce_scatter x1 -> x0, waiting for transfers between devices: 72.6 us -> none  [per_device(): lax.psum_scatter(running_total, 'tm', scatter_dimension=1, tiled=True)]
    pallas_call x0 -> x5, Pallas kernels: none -> 52.3 us  [the longest x4 49 us: spectrum(): pl.pallas_call(functools.partial(spectrum_kernel, tiles, step), grid_spec...]
    all_to_all x2 -> x4, starting transfers between devices: 73.9 us -> 30.2 us  [per_device(): lax.all_to_all(mine, 'tm', 0, 0, axis_index_groups=places, tiled=True)]
    reduce_sum x6 -> x1, other arithmetic: 35.2 us -> 0.85 us  [window_tables(): energy = jnp.sum(window * window)]
    unnamed x17 -> x10, local copies, waits for them, and re-layouts: 33.8 us -> 1.76 us
    ppermute x1 -> x15, starting transfers between devices: 1.28 us -> 28.5 us  [the longest x4 16.4 us: per_device(): lax.ppermute(x[12 + first:12 + first + tiles, HALF * TILE:], 'tm', to_right)]
    all_to_all x2 -> x4, waiting for transfers between devices: 10.6 us -> 34.3 us  [per_device(): lax.all_to_all(mine, 'tm', 0, 0, axis_index_groups=places, tiled=True)]
  transfers between devices with their start and end apart: 4 -> 19, of which waited for: 4 -> 5; matrix products, arithmetic and copies ran while one was open for 1% -> 9% of each run, Pallas kernels for 0% -> 21%
where the time goes in v1:
time: 175 us; the launch traced here: 174 us
  starting transfers between devices  58.8 us (34%)
  Pallas kernels  52.3 us (30%)
  waiting for transfers between devices  37.9 us (22%)
  other arithmetic  13.7 us (8%)
  local copies, waits for them, and re-layouts  9.75 us (6%)
    pallas_call x4, Pallas kernels, spectrum(): pl.pallas_call(functools.partial(spectrum_kernel, tiles, step), grid_spec...  49 us
    all_to_all x4, waiting for transfers between devices, per_device(): lax.all_to_all(mine, 'tm', 0, 0, axis_index_groups=places, tiled=True)  34.3 us
    all_to_all x4, starting transfers between devices, per_device(): lax.all_to_all(mine, 'tm', 0, 0, axis_index_groups=places, tiled=True)  30.2 us
    ppermute x4, starting transfers between devices, per_device(): lax.ppermute(x[12 + first:12 + first + tiles, HALF * TILE:], 'tm', to_right)  16.4 us
    add x4, other arithmetic, per_device(): mine = own + lax.ppermute(other, 'tm', swap)  8.7 us
    ppermute x3, starting transfers between devices, per_device(): lax.ppermute(band_sum, 'chan', [(i, (i + shift) % chans) for i in range(c...  5.83 us
    ppermute x4, starting transfers between devices, per_device(): left = lax.ppermute(x[first:first + tiles, :HALF * TILE], 'tm', to_left)  5.12 us
    slice x1, local copies, waits for them, and re-layouts, per_device(): x[12 + first:12 + first + tiles, HALF * TILE:]  4.73 us
  transfers between devices with their start and end apart: 19, of which 5 were waited for; matrix products, arithmetic and copies ran while one was open for 9% of the time, Pallas kernels for 21%

profile of v1, /device:TPU:0, one launch (start us, length us, event | category | flops | bytes accessed | tf_op | source)
XLA Modules:
  0.0 174.0 jit_solution(140419108529272787)
XLA Ops:
  0.6 4.7 %fusion.1 = (f32[3,512,128]{2,1,0:T(8,128)}, f32[3,512,128]{2,1,0:T(8,128)}, f32[3,512,128]{2,1,0:T(8,128)}, f32[3,512,128]{2,1,0:T(8,128)}, f32[3,512,128]{2,1,...) fusion(f32[24,1024,128]{2,1,0:T(8,128)} %bitcast.15), kind=kLoop, calls=%fused_computation.11 | loop fusion | bytes 12582912 | tf_op jit(solution)/shard_map/slice | solution.py:320
  6.6 3.9 %collective-permute-start.7 = (f32[3,512,128]{2,1,0:T(8,128)}, f32[3,512,128]{2,1,0:T(8,128)}, u32[]{:S(2)}, u32[]{:S(2)}) collective-permute-start(f32[3,512,128]{2,1,0:T(8,128)} %get-tuple-element.33), channel_id=1, source_target_pairs={{0,1},{1,2},{2,3},{3,4},{4,5},{5,6},{6,7},{7,8},{8,9},{9,10},{10,1... | collective-permute-start | bytes 2359304 | tf_op jit(solution)/shard_map/ppermute | solution.py:320
  11.9 3.9 %collective-permute-start.5 = (f32[3,512,128]{2,1,0:T(8,128)}, f32[3,512,128]{2,1,0:T(8,128)}, u32[]{:S(2)}, u32[]{:S(2)}) collective-permute-start(f32[3,512,128]{2,1,0:T(8,128)} %get-tuple-element.35), channel_id=1, source_target_pairs={{0,1},{1,2},{2,3},{3,4},{4,5},{5,6},{6,7},{7,8},{8,9},{9,10},{10,1... | collective-permute-start | bytes 2359304 | tf_op jit(solution)/shard_map/ppermute | solution.py:320
  17.1 4.6 %collective-permute-start.3 = (f32[3,512,128]{2,1,0:T(8,128)S(1)}, f32[3,512,128]{2,1,0:T(8,128)}, u32[]{:S(2)}, u32[]{:S(2)}) collective-permute-start(f32[3,512,128]{2,1,0:T(8,128)S(1)} %get-tuple-element.37), channel_id=1, source_target_pairs={{0,1},{1,2},{2,3},{3,4},{4,5},{5,6},{6,7},{7,8},{8,9},{9,10},{10,1... | collective-permute-start | bytes 2359304 | tf_op jit(solution)/shard_map/ppermute | solution.py:320
  24.1 12.2 %spectrum.4 = (f32[16,12,8,128]{3,2,1,0:T(8,128)}, f32[16,12,8,128]{3,2,1,0:T(8,128)}, f32[8,128]{1,0:T(8,128)}) custom-call(s32[4]{0:T(128)} %pad_add_fusion.meta, f32[24,1024,128]{2,1,0:T(8,128)} %bitcast.16, f32[3,512,128]{2,1,0:T(8,128)} %collective-permute-done.6.left_ref, f32[3,512,128]{2,1,0:T(8,128)} %collective-permute-done.7.right_ref, ...), custom_call_target="tpu_custom_call" | custom-call | tf_op jit(solution)/shard_map/spectrum/pallas_call | solution.py:208
  36.4 12.3 %spectrum.5 = (f32[16,12,8,128]{3,2,1,0:T(8,128)}, f32[16,12,8,128]{3,2,1,0:T(8,128)}, f32[8,128]{1,0:T(8,128)}) custom-call(s32[4]{0:T(128)} %pad_add_fusion.meta, f32[24,1024,128]{2,1,0:T(8,128)} %bitcast.17, f32[3,512,128]{2,1,0:T(8,128)} %collective-permute-done.4.left_ref, f32[3,512,128]{2,1,0:T(8,128)} %collective-permute-done.5.right_ref, ...), custom_call_target="tpu_custom_call" | custom-call | tf_op jit(solution)/shard_map/spectrum/pallas_call | solution.py:208
  48.7 12.3 %spectrum.6 = (f32[16,12,8,128]{3,2,1,0:T(8,128)}, f32[16,12,8,128]{3,2,1,0:T(8,128)}, f32[8,128]{1,0:T(8,128)}) custom-call(s32[4]{0:T(128)} %pad_add_fusion.meta, f32[24,1024,128]{2,1,0:T(8,128)} %bitcast.18, f32[3,512,128]{2,1,0:T(8,128)} %collective-permute-done.2.left_ref, f32[3,512,128]{2,1,0:T(8,128)} %collective-permute-done.3.right_ref, ...), custom_call_target="tpu_custom_call" | custom-call | tf_op jit(solution)/shard_map/spectrum/pallas_call | solution.py:208
  62.7 3.9 %collective-permute-start.1 = (f32[3,512,128]{2,1,0:T(8,128)S(1)}, f32[3,512,128]{2,1,0:T(8,128)}, u32[]{:S(2)}, u32[]{:S(2)}) collective-permute-start(f32[3,512,128]{2,1,0:T(8,128)S(1)} %get-tuple-element.39), channel_id=1, source_target_pairs={{0,1},{1,2},{2,3},{3,4},{4,5},{5,6},{6,7},{7,8},{8,9},{9,10},{10,1... | collective-permute-start | bytes 2359304 | tf_op jit(solution)/shard_map/ppermute | solution.py:320
  67.2 2.1 %add.38 = f32[16,12,8,128]{3,2,1,0:T(8,128)} add(f32[16,12,8,128]{3,2,1,0:T(8,128)} %get-tuple-element.28, f32[16,12,8,128]{3,2,1,0:T(8,128)S(1)} %collective-permute-done.11) | non-fusion elementwise | flops 196608 | bytes 2359296 | tf_op jit(solution)/shard_map/add | solution.py:337
  69.3 15.8 %all-to-all-start.3 = ((f32[16,12,8,128]{3,2,1,0:T(8,128)}), f32[16,12,8,128]{3,2,1,0:T(8,128)S(1)}, u32[]{:S(2)}, u32[]{:S(2)}) async-start(f32[16,12,8,128]{3,2,1,0:T(8,128)} %add.38), calls=%async_computation.3 | async-start | bytes 1572864 | tf_op jit(solution)/shard_map/all_to_all | solution.py:338
  86.0 12.2 %spectrum.7 = (f32[16,12,8,128]{3,2,1,0:T(8,128)}, f32[16,12,8,128]{3,2,1,0:T(8,128)}, f32[8,128]{1,0:T(8,128)}) custom-call(s32[4]{0:T(128)} %pad_add_fusion.meta, f32[24,1024,128]{2,1,0:T(8,128)} %bitcast.19, f32[3,512,128]{2,1,0:T(8,128)} %copy-done.4, f32[3,512,128]{2,1,0:T(8,128)} %collective-permute-done.1.right_ref, ...), custom_call_target="tpu_custom_call" | custom-call | tf_op jit(solution)/shard_map/spectrum/pallas_call | solution.py:208
  100.2 2.4 %add.37 = f32[16,12,8,128]{3,2,1,0:T(8,128)} add(f32[16,12,8,128]{3,2,1,0:T(8,128)} %get-tuple-element.26, f32[16,12,8,128]{3,2,1,0:T(8,128)} %collective-permute-done.10) | non-fusion elementwise | flops 196608 | bytes 2359296 | tf_op jit(solution)/shard_map/add | solution.py:337
  102.5 7.2 %all-to-all-start.2 = ((f32[16,12,8,128]{3,2,1,0:T(8,128)}), f32[16,12,8,128]{3,2,1,0:T(8,128)S(1)}, u32[]{:S(2)}, u32[]{:S(2)}) async-start(f32[16,12,8,128]{3,2,1,0:T(8,128)} %add.37), calls=%async_computation.2 | async-start | bytes 1572864 | tf_op jit(solution)/shard_map/all_to_all | solution.py:338
  109.8 2.1 %fusion = f32[16,13,8,128]{3,2,1,0:T(8,128)} fusion(f32[16,13,8,128]{3,2,1,0:T(8,128)S(1)} %collective-permute-done.8, f32[16,1,8,128]{3,2,1,0:T(8,128)S(1)} %broadcast_in_dim.8, f32[16,12,8,128]{3,2,1,0:T(8,128)} %get-tuple-element.21), kind=kLoop, calls=%fused_computation.2 | loop fusion | flops 425984 | bytes 2555904 | tf_op jit(solution)/shard_map/add | solution.py:337
  111.9 12.9 %all-to-all-done.2.refs_1_ = f32[16,12,8,128]{3,2,1,0:T(8,128)S(1)} async-done(((f32[16,12,8,128]{3,2,1,0:T(8,128)}), f32[16,12,8,128]{3,2,1,0:T(8,128)S(1)}, u32[]{:S(2)}, u32[]{:S(2)}) %all-to-all-start.2) | async-done | bytes 786464 | tf_op jit(solution)/shard_map/all_to_all | solution.py:338
  124.8 3.6 %all-to-all-start = ((f32[16,13,8,128]{3,2,1,0:T(8,128)}), f32[16,13,8,128]{3,2,1,0:T(8,128)S(1)}, u32[]{:S(2)}, u32[]{:S(2)}) async-start(f32[16,13,8,128]{3,2,1,0:T(8,128)} %fusion), calls=%async_computation | async-start | bytes 1703936 | tf_op jit(solution)/shard_map/all_to_all | solution.py:338
  128.5 2.5 %collective-permute-done.9 = f32[16,12,8,128]{3,2,1,0:T(8,128)S(1)} collective-permute-done((f32[16,12,8,128]{3,2,1,0:T(8,128)}, f32[16,12,8,128]{3,2,1,0:T(8,128)S(1)}, u32[]{:S(2)}, u32[]{:S(2)}) %collective-permute-start.9) | collective-permute-done | bytes 786464 | tf_op jit(solution)/shard_map/ppermute | solution.py:337
  131.0 2.1 %add.36 = f32[16,12,8,128]{3,2,1,0:T(8,128)} add(f32[16,12,8,128]{3,2,1,0:T(8,128)} %get-tuple-element.24, f32[16,12,8,128]{3,2,1,0:T(8,128)S(1)} %collective-permute-done.9) | non-fusion elementwise | flops 196608 | bytes 2359296 | tf_op jit(solution)/shard_map/add | solution.py:337
  133.1 10.0 %all-to-all-done.refs_3_ = f32[16,13,8,128]{3,2,1,0:T(8,128)S(1)} async-done(((f32[16,13,8,128]{3,2,1,0:T(8,128)}), f32[16,13,8,128]{3,2,1,0:T(8,128)S(1)}, u32[]{:S(2)}, u32[]{:S(2)}) %all-to-all-start) | async-done | bytes 852000 | tf_op jit(solution)/shard_map/all_to_all | solution.py:338
  143.1 3.6 %all-to-all-start.1 = ((f32[16,12,8,128]{3,2,1,0:T(8,128)}), f32[16,12,8,128]{3,2,1,0:T(8,128)S(1)}, u32[]{:S(2)}, u32[]{:S(2)}) async-start(f32[16,12,8,128]{3,2,1,0:T(8,128)} %add.36), calls=%async_computation.1 | async-start | bytes 1572864 | tf_op jit(solution)/shard_map/all_to_all | solution.py:338
  148.9 11.4 %all-to-all-done.1.refs_0_ = f32[16,12,8,128]{3,2,1,0:T(8,128)S(1)} async-done(((f32[16,12,8,128]{3,2,1,0:T(8,128)}), f32[16,12,8,128]{3,2,1,0:T(8,128)S(1)}, u32[]{:S(2)}, u32[]{:S(2)}) %all-to-all-start.1) | async-done | bytes 786464 | tf_op jit(solution)/shard_map/all_to_all | solution.py:338
  161.1 3.3 %finish.1 = (f32[192,256]{1,0:T(8,128)}, f32[1,256]{1,0:T(1,128)}, f32[24,8]{1,0:T(8,128)}) custom-call(s32[4]{0:T(128)} %pad_add_fusion.meta, f32[1]{0:T(128)} %bitcast.4.scale_ref, f32[2,256,128]{2,1,0:T(8,128)} %constant.61.clone.pick_ref, f32[16,8,128]{2,1,0:T(8,128)} %slice_bitcast_fusion.edges_ref, f32[16,12,8,128]{3,2,1,0:T(8,128)} %copy-done.3, ...), custom_call_target="tpu_custom_call" | custom-call | tf_op jit(solution)/shard_map/finish/pallas_call | solution.py:289
  164.5 1.6 collective-permute-start.12
  166.1 2.9 %collective-permute-start.13 = (f32[1,256]{1,0:T(1,128)}, f32[1,256]{1,0:T(1,128)S(1)}, u32[]{:S(2)}, u32[]{:S(2)}) collective-permute-start(f32[1,256]{1,0:T(1,128)} %get-tuple-element.32), channel_id=1, source_target_pairs={{0,64},{32,96},{64,0},{96,32},{1,65},{33,97},{65,1},{97,33},{2,66}... | collective-permute-start | bytes 3080 | tf_op jit(solution)/shard_map/ppermute | solution.py:344
  (47 shorter events, 18.8 us)
Async XLA Ops:
  5.4 11.8 %collective-permute-start.6 = (f32[3,512,128]{2,1,0:T(8,128)}, f32[3,512,128]{2,1,0:T(8,128)}, u32[]{:S(2)}, u32[]{:S(2)}) collective-permute-start(f32[3,512,128]{2,1,0:T(8,128)} %get-tuple-element.34), channel_id=1, source_target_pairs={{1,0},{2,1},{3,2},{4,3},{5,4},{6,5},{7,6},{8,7},{9,8},{10,9},{11,1... | collective-permute-start | bytes 2359304 | tf_op jit(solution)/shard_map/ppermute | solution.py:319
  6.6 16.9 %collective-permute-start.7 = (f32[3,512,128]{2,1,0:T(8,128)}, f32[3,512,128]{2,1,0:T(8,128)}, u32[]{:S(2)}, u32[]{:S(2)}) collective-permute-start(f32[3,512,128]{2,1,0:T(8,128)} %get-tuple-element.33), channel_id=1, source_target_pairs={{0,1},{1,2},{2,3},{3,4},{4,5},{5,6},{6,7},{7,8},{8,9},{9,10},{10,1... | collective-permute-start | bytes 2359304 | tf_op jit(solution)/shard_map/ppermute | solution.py:320
  10.6 25.8 %collective-permute-start.4 = (f32[3,512,128]{2,1,0:T(8,128)}, f32[3,512,128]{2,1,0:T(8,128)}, u32[]{:S(2)}, u32[]{:S(2)}) collective-permute-start(f32[3,512,128]{2,1,0:T(8,128)} %get-tuple-element.36), channel_id=1, source_target_pairs={{1,0},{2,1},{3,2},{4,3},{5,4},{6,5},{7,6},{8,7},{9,8},{10,9},{11,1... | collective-permute-start | bytes 2359304 | tf_op jit(solution)/shard_map/ppermute | solution.py:319
  11.9 24.5 %collective-permute-start.5 = (f32[3,512,128]{2,1,0:T(8,128)}, f32[3,512,128]{2,1,0:T(8,128)}, u32[]{:S(2)}, u32[]{:S(2)}) collective-permute-start(f32[3,512,128]{2,1,0:T(8,128)} %get-tuple-element.35), channel_id=1, source_target_pairs={{0,1},{1,2},{2,3},{3,4},{4,5},{5,6},{6,7},{7,8},{8,9},{9,10},{10,1... | collective-permute-start | bytes 2359304 | tf_op jit(solution)/shard_map/ppermute | solution.py:320
  15.8 32.8 %collective-permute-start.2 = (f32[3,512,128]{2,1,0:T(8,128)S(1)}, f32[3,512,128]{2,1,0:T(8,128)}, u32[]{:S(2)}, u32[]{:S(2)}) collective-permute-start(f32[3,512,128]{2,1,0:T(8,128)S(1)} %get-tuple-element.38), channel_id=1, source_target_pairs={{1,0},{2,1},{3,2},{4,3},{5,4},{6,5},{7,6},{8,7},{9,8},{10,9},{11,1... | collective-permute-start | bytes 2359304 | tf_op jit(solution)/shard_map/ppermute | solution.py:319
  17.1 31.5 %collective-permute-start.3 = (f32[3,512,128]{2,1,0:T(8,128)S(1)}, f32[3,512,128]{2,1,0:T(8,128)}, u32[]{:S(2)}, u32[]{:S(2)}) collective-permute-start(f32[3,512,128]{2,1,0:T(8,128)S(1)} %get-tuple-element.37), channel_id=1, source_target_pairs={{0,1},{1,2},{2,3},{3,4},{4,5},{5,6},{6,7},{7,8},{8,9},{9,10},{10,1... | collective-permute-start | bytes 2359304 | tf_op jit(solution)/shard_map/ppermute | solution.py:320
  60.9 6.2 %collective-permute-start.11 = (f32[16,12,8,128]{3,2,1,0:T(8,128)}, f32[16,12,8,128]{3,2,1,0:T(8,128)S(1)}, u32[]{:S(2)}, u32[]{:S(2)}) collective-permute-start(f32[16,12,8,128]{3,2,1,0:T(8,128)} %get-tuple-element.29), channel_id=1, source_target_pairs={{0,1},{1,0},{2,3},{3,2},{4,5},{5,4},{6,7},{7,6},{8,9},{9,8},{10,11... | collective-permute-start | bytes 2359304 | tf_op jit(solution)/shard_map/ppermute | solution.py:337
  61.4 23.6 %collective-permute-start = (f32[3,512,128]{2,1,0:T(8,128)S(1)}, f32[3,512,128]{2,1,0:T(8,128)S(1)}, u32[]{:S(2)}, u32[]{:S(2)}) collective-permute-start(f32[3,512,128]{2,1,0:T(8,128)S(1)} %get-tuple-element.40), channel_id=1, source_target_pairs={{1,0},{2,1},{3,2},{4,3},{5,4},{6,5},{7,6},{8,7},{9,8},{10,9},{11,1... | collective-permute-start | bytes 2359304 | tf_op jit(solution)/shard_map/ppermute | solution.py:319
  62.7 22.4 %collective-permute-start.1 = (f32[3,512,128]{2,1,0:T(8,128)S(1)}, f32[3,512,128]{2,1,0:T(8,128)}, u32[]{:S(2)}, u32[]{:S(2)}) collective-permute-start(f32[3,512,128]{2,1,0:T(8,128)S(1)} %get-tuple-element.39), channel_id=1, source_target_pairs={{0,1},{1,2},{2,3},{3,4},{4,5},{5,6},{6,7},{7,8},{8,9},{9,10},{10,1... | collective-permute-start | bytes 2359304 | tf_op jit(solution)/shard_map/ppermute | solution.py:320
  66.7 33.5 %collective-permute-start.10 = (f32[16,12,8,128]{3,2,1,0:T(8,128)}, f32[16,12,8,128]{3,2,1,0:T(8,128)}, u32[]{:S(2)}, u32[]{:S(2)}) collective-permute-start(f32[16,12,8,128]{3,2,1,0:T(8,128)} %get-tuple-element.27), channel_id=1, source_target_pairs={{0,1},{1,0},{2,3},{3,2},{4,5},{5,4},{6,7},{7,6},{8,9},{9,8},{10,11... | collective-permute-start | bytes 2359304 | tf_op jit(solution)/shard_map/ppermute | solution.py:337
  69.3 33.3 %all-to-all-start.3 = ((f32[16,12,8,128]{3,2,1,0:T(8,128)}), f32[16,12,8,128]{3,2,1,0:T(8,128)S(1)}, u32[]{:S(2)}, u32[]{:S(2)}) async-start(f32[16,12,8,128]{3,2,1,0:T(8,128)} %add.38), calls=%async_computation.3 | async-start | bytes 1572864 | tf_op jit(solution)/shard_map/all_to_all | solution.py:338
  85.1 0.9 copy-start.4
  100.1 9.7 %collective-permute-start.8 = (f32[16,13,8,128]{3,2,1,0:T(8,128)S(1)}, f32[16,13,8,128]{3,2,1,0:T(8,128)S(1)}, u32[]{:S(2)}, u32[]{:S(2)}) collective-permute-start(f32[16,13,8,128]{3,2,1,0:T(8,128)S(1)} %pad_maximum_fusion), channel_id=1, source_target_pairs={{0,1},{1,0},{2,3},{3,2},{4,5},{5,4},{6,7},{7,6},{8,9},{9,8},{10,11... | collective-permute-start | bytes 2555912 | tf_op jit(solution)/shard_map/ppermute | solution.py:337
  102.5 57.7 %copy-start.1 = (f32[16,12,8,128]{3,2,1,0:T(8,128)}, f32[16,12,8,128]{3,2,1,0:T(8,128)S(1)}, u32[]{:S(2)}) copy-start(f32[16,12,8,128]{3,2,1,0:T(8,128)S(1)} %all-to-all-done.3.refs_2_) | copy-start | bytes 2359300
  102.5 22.2 %all-to-all-start.2 = ((f32[16,12,8,128]{3,2,1,0:T(8,128)}), f32[16,12,8,128]{3,2,1,0:T(8,128)S(1)}, u32[]{:S(2)}, u32[]{:S(2)}) async-start(f32[16,12,8,128]{3,2,1,0:T(8,128)} %add.37), calls=%async_computation.2 | async-start | bytes 1572864 | tf_op jit(solution)/shard_map/all_to_all | solution.py:338
  124.8 35.5 %copy-start.2 = (f32[16,12,8,128]{3,2,1,0:T(8,128)}, f32[16,12,8,128]{3,2,1,0:T(8,128)S(1)}, u32[]{:S(2)}) copy-start(f32[16,12,8,128]{3,2,1,0:T(8,128)S(1)} %all-to-all-done.2.refs_1_) | copy-start | bytes 2359300
  124.8 18.4 %all-to-all-start = ((f32[16,13,8,128]{3,2,1,0:T(8,128)}), f32[16,13,8,128]{3,2,1,0:T(8,128)S(1)}, u32[]{:S(2)}, u32[]{:S(2)}) async-start(f32[16,13,8,128]{3,2,1,0:T(8,128)} %fusion), calls=%async_computation | async-start | bytes 1703936 | tf_op jit(solution)/shard_map/all_to_all | solution.py:338
  128.4 2.6 %collective-permute-start.9 = (f32[16,12,8,128]{3,2,1,0:T(8,128)}, f32[16,12,8,128]{3,2,1,0:T(8,128)S(1)}, u32[]{:S(2)}, u32[]{:S(2)}) collective-permute-start(f32[16,12,8,128]{3,2,1,0:T(8,128)} %get-tuple-element.25), channel_id=1, source_target_pairs={{0,1},{1,0},{2,3},{3,2},{4,5},{5,4},{6,7},{7,6},{8,9},{9,8},{10,11... | collective-permute-start | bytes 2359304 | tf_op jit(solution)/shard_map/ppermute | solution.py:337
  143.1 17.1 %copy-start = (f32[16,13,8,128]{3,2,1,0:T(8,128)}, f32[16,13,8,128]{3,2,1,0:T(8,128)S(1)}, u32[]{:S(2)}) copy-start(f32[16,13,8,128]{3,2,1,0:T(8,128)S(1)} %all-to-all-done.refs_3_) | copy-start | bytes 2555908
  143.1 17.1 %all-to-all-start.1 = ((f32[16,12,8,128]{3,2,1,0:T(8,128)}), f32[16,12,8,128]{3,2,1,0:T(8,128)S(1)}, u32[]{:S(2)}, u32[]{:S(2)}) async-start(f32[16,12,8,128]{3,2,1,0:T(8,128)} %add.36), calls=%async_computation.1 | async-start | bytes 1572864 | tf_op jit(solution)/shard_map/all_to_all | solution.py:338
  160.3 0.9 copy-start.3
  164.5 7.2 %collective-permute-start.12 = (f32[1,256]{1,0:T(1,128)}, f32[1,256]{1,0:T(1,128)S(1)}, u32[]{:S(2)}, u32[]{:S(2)}) collective-permute-start(f32[1,256]{1,0:T(1,128)} %get-tuple-element.32), channel_id=1, source_target_pairs={{0,32},{32,64},{64,96},{96,0},{1,33},{33,65},{65,97},{97,1},{2,34}... | collective-permute-start | bytes 3080 | tf_op jit(solution)/shard_map/ppermute | solution.py:344
  166.1 5.6 %collective-permute-start.13 = (f32[1,256]{1,0:T(1,128)}, f32[1,256]{1,0:T(1,128)S(1)}, u32[]{:S(2)}, u32[]{:S(2)}) collective-permute-start(f32[1,256]{1,0:T(1,128)} %get-tuple-element.32), channel_id=1, source_target_pairs={{0,64},{32,96},{64,0},{96,32},{1,65},{33,97},{65,1},{97,33},{2,66}... | collective-permute-start | bytes 3080 | tf_op jit(solution)/shard_map/ppermute | solution.py:344
  169.0 3.8 %collective-permute-start.14 = (f32[1,256]{1,0:T(1,128)}, f32[1,256]{1,0:T(1,128)S(1)}, u32[]{:S(2)}, u32[]{:S(2)}) collective-permute-start(f32[1,256]{1,0:T(1,128)} %get-tuple-element.32), channel_id=1, source_target_pairs={{0,96},{32,0},{64,32},{96,64},{1,97},{33,1},{65,33},{97,65},{2,98}... | collective-permute-start | bytes 3080 | tf_op jit(solution)/shard_map/ppermute | solution.py:344

commit v2 on v1

v2 whole, which is shorter than its diff:
```python
import functools

import jax
import jax.numpy as jnp
import numpy as np
from jax import lax
from jax.experimental import pallas as pl
from jax.experimental.pallas import tpu as pltpu
from jax.sharding import PartitionSpec as P


SEG = 16384
ROOT = 128
HALF = ROOT // 2
TILE = 8
LANES = 128
STEPS = 3
SIDE = 12
PLACES = 32
SEGS = 4
COST = 1 << 22


def split_bf16(table):
    high = table.astype(jnp.bfloat16)
    low = (table - high.astype(np.float64)).astype(jnp.bfloat16)
    return high, low


def dft_constants():
    n = np.arange(ROOT)
    angle = 2.0 * np.pi * ((n[:, None] * n[None, :]) % ROOT) / ROOT
    rows = np.arange(HALF)
    first = np.concatenate([np.cos(angle[:HALF]), -np.sin(angle[:HALF])], axis=0)
    first[HALF] = 1.0 - 2.0 * (n % 2)
    high, low = split_bf16(first)
    first_high = np.concatenate([high, high], axis=1)
    twist = 2.0 * np.pi * (rows[:, None] * n[None, :]) / SEG
    cos_twist = np.cos(twist)
    cos_imag = cos_twist.copy()
    cos_imag[0] = 0.0
    twiddle = np.stack([cos_twist, cos_imag, np.sin(twist)]).astype(np.float32)
    edge = np.pi * n / ROOT
    edge_twiddle = np.stack([np.cos(edge), -np.sin(edge)]).astype(np.float32)
    columns = []
    for k in range(HALF):
        columns += [k, ROOT - 1 - k]
    c = np.cos(angle[:, columns])
    s = np.sin(angle[:, columns])
    high, low_second = split_bf16(np.block([[c, -s], [s, c]]))
    second = np.concatenate([high, high, low_second], axis=0)
    return first_high, low, twiddle, edge_twiddle, second


def window_table():
    pos = jnp.arange(SEG, dtype=jnp.float32)
    window = 0.5 - 0.5 * jnp.cos(2.0 * jnp.pi * pos / SEG)
    energy = jnp.sum(window * window)
    return window.reshape(ROOT, LANES), energy


def spectrum_kernel(
    tiles,
    first,
    last,
    meta,
    x_hbm,
    remote_hbm,
    halo_a_hbm,
    halo_b_hbm,
    window_ref,
    first_ref,
    first_low_ref,
    twiddle_ref,
    edge_ref,
    second_ref,
    edges_in_ref,
    out_ref,
    edges_ref,
    x_buf,
    means,
    spec,
    corner,
    result,
    sems,
):
    group = pl.program_id(0)
    core = meta[0]
    near = pl.multiple_of(HALF + ROOT * core, HALF)
    far = pl.multiple_of(HALF + ROOT * (1 - core), HALF)

    def loads(place, tile, halo_hbm, halo_tile, right):
        at = pl.multiple_of(right * (5 * HALF), HALF)
        out = []
        for c in range(TILE):
            out.append((x_hbm.at[core * SIDE + tile, :, c, 0, :], x_buf.at[place, c, pl.ds(near, ROOT), :]))
            out.append((remote_hbm.at[tile, :, c, 0, :], x_buf.at[place, c, pl.ds(far, ROOT), :]))
            out.append((halo_hbm.at[halo_tile, :, c, 0, :], x_buf.at[place, c, pl.ds(at, HALF), :]))
        return [
            pltpu.make_async_copy(src, dst, sems.at[place, k]) for k, (src, dst) in enumerate(out)
        ]

    @pl.when(group == 0)
    def _():
        for u in range(tiles):
            for copy in loads(u, first + u, halo_a_hbm, u, 1 - core):
                copy.start()
        for u in range(tiles):
            for copy in loads(tiles + u, SIDE // 2 + first + u, halo_b_hbm, u, core):
                copy.start()
        edges_ref[...] = edges_in_ref[...]

    right = jnp.where(group == 0, 1 - core, core)
    keep = jnp.where(right == 1, meta[1], meta[2]).astype(jnp.float32)
    base = group * tiles
    outer_at = pl.multiple_of(right * (5 * HALF), HALF)
    outer_start = pl.multiple_of(right * (4 * HALF), HALF)
    starts = (HALF, 2 * HALF, 3 * HALF, outer_start)

    def wait_for(u):
        for copy in loads(base + u, first + u, halo_a_hbm, u, right):
            copy.wait()

    def average(u):
        def part(c, at):
            return jnp.sum(x_buf[base + u, c, pl.ds(at, HALF), :].reshape(HALF // TILE, TILE, LANES), axis=0)

        sums = [[] for _ in range(SEGS)]
        for c in range(TILE):
            q = [part(c, HALF * (k + 1)) for k in range(4)]
            outer = part(c, outer_at) + jnp.where(right == 1, q[3], q[0])
            for k, value in enumerate((q[0] + q[1], q[1] + q[2], q[2] + q[3], outer)):
                sums[k].append(value)
        both = jnp.stack(sum(sums, []))
        total = jnp.sum(jnp.sum(both, axis=1), axis=1, keepdims=True) * (1.0 / SEG)
        means[u] = jnp.broadcast_to(total, (SEGS * TILE, LANES))

    def put(u, row, size, part, value):
        high = value.astype(jnp.bfloat16)
        lanes = slice(part * LANES, (part + 1) * LANES)
        lanes_low = slice((2 + part) * LANES, (3 + part) * LANES)
        spec[u, row : row + size, lanes] = high
        spec[u, row : row + size, lanes_low] = (value - high.astype(jnp.float32)).astype(jnp.bfloat16)

    def forward(u):
        for pair in range(TILE // 2):
            for seg in range(SEGS):
                highs = []
                lows = []
                for c in (2 * pair, 2 * pair + 1):
                    r = seg * TILE + c
                    piece = x_buf[base + u, c, pl.ds(starts[seg], ROOT), :]
                    centred = (piece - means[u, r : r + 1, :]) * window_ref[...]
                    high = centred.astype(jnp.bfloat16)
                    highs.append(high)
                    lows.append((centred - high.astype(jnp.float32)).astype(jnp.bfloat16))
                high = jnp.concatenate(highs, axis=1)
                low = jnp.concatenate(lows, axis=1)
                stage = jnp.dot(
                    first_ref[...], jnp.concatenate([high, low], axis=0), preferred_element_type=jnp.float32
                ) + jnp.dot(first_low_ref[...], high, preferred_element_type=jnp.float32)
                for q in range(2):
                    r = seg * TILE + 2 * pair + q
                    real = stage[:HALF, q * LANES : (q + 1) * LANES]
                    imag = stage[HALF:, q * LANES : (q + 1) * LANES]
                    corner[u, r : r + 1, :] = imag[0:1]
                    put(u, r * HALF, HALF, 0, real * twiddle_ref[0] + imag * twiddle_ref[2])
                    put(u, r * HALF, HALF, 1, imag * twiddle_ref[1] - real * twiddle_ref[2])

    rows = SEGS * TILE * HALF

    def second(u):
        for part in range(2):
            put(u, rows, SEGS * TILE, part, corner[u] * edge_ref[part : part + 1])
        result[u] = jnp.dot(
            spec[u], second_ref[: 4 * LANES, :], preferred_element_type=jnp.float32
        ) + jnp.dot(spec[u, :, : 2 * LANES], second_ref[4 * LANES :, :], preferred_element_type=jnp.float32)

    row_id = lax.broadcasted_iota(jnp.int32, (HALF, LANES), 0)
    lane_id = lax.broadcasted_iota(jnp.int32, (HALF, LANES), 1)
    replaced = (row_id == 0) & (lane_id % 2 == 1)
    tile_lane = lax.broadcasted_iota(jnp.int32, (TILE, LANES), 1)
    tile_row = lax.broadcasted_iota(jnp.int32, (TILE, LANES), 0)
    lower_rows = tile_row < TILE // 2

    def emit(u):
        def power_of(start, size):
            real = result[u, start : start + size, :LANES]
            imag = result[u, start : start + size, LANES:]
            return real * real + imag * imag

        def all_segments(start, step, size):
            inner = power_of(start, size) + power_of(start + step, size) + power_of(start + 2 * step, size)
            return inner + keep * power_of(start + 3 * step, size)

        edge_power = all_segments(rows, TILE, TILE)
        edge_tile = jnp.zeros((TILE, LANES), jnp.float32)
        columns = []
        for pair in range(TILE // 2):
            blocks = []
            for q in range(2):
                c = 2 * pair + q
                total = all_segments(c * HALF, TILE * HALF, HALF)
                edge_tile = jnp.where(tile_row == c, total[0:1], edge_tile)
                blocks.append(jnp.where(replaced, edge_power[c : c + 1], total))
            columns.append(jnp.concatenate(blocks, axis=0).T)
        edge_value = jnp.sum(jnp.where(tile_lane == LANES - 1, edge_tile, 0.0), axis=1, keepdims=True)
        tile_number = group * (SIDE // 2) + first + u
        edges_ref[...] = jnp.where(tile_lane == tile_number, edge_value, edges_ref[...])
        at = 2 * (base + u)
        for half in range(2):
            a, b = columns[2 * half], columns[2 * half + 1]
            for place in range(PLACES // 2):
                va = a[place * TILE : (place + 1) * TILE]
                vb = b[place * TILE : (place + 1) * TILE]
                out_ref[2 * place, at + half] = jnp.where(lower_rows, va, pltpu.roll(vb, 4, 0))
                out_ref[2 * place + 1, at + half] = jnp.where(lower_rows, pltpu.roll(va, 4, 0), vb)

    for u in range(tiles):
        wait_for(u)
    for u in range(tiles):
        average(u)
    for u in range(tiles):
        forward(u)
        second(u)
        if u > 0:
            emit(u - 1)
    emit(tiles - 1)
    if last:

        @pl.when(group == 1)
        def _():
            for place in range(PLACES):
                out_ref[place, 4 * tiles] = edges_ref[...]


def spectrum(first, tiles, last, meta, x, remote, halo_a, halo_b, window, constants, edges):
    first_high, first_low, twiddle, edge_twiddle, second = constants
    whole = lambda shape: pl.BlockSpec(shape, lambda i, m: (0,) * len(shape))
    hbm = pl.BlockSpec(memory_space=pl.ANY)
    out_shape = (PLACES, 4 * tiles + int(last), TILE, LANES)
    rows = SEGS * TILE * (HALF + 1)
    by_channel = lambda v: v.reshape(-1, v.shape[1] // TILE, TILE, 1, LANES)
    work = 2 * tiles * SEGS * TILE
    return pl.pallas_call(
        functools.partial(spectrum_kernel, tiles, first, last),
        grid_spec=pltpu.PrefetchScalarGridSpec(
            num_scalar_prefetch=1,
            grid=(2,),
            in_specs=[
                hbm,
                hbm,
                hbm,
                hbm,
                whole((ROOT, LANES)),
                whole((ROOT, 2 * LANES)),
                whole((ROOT, LANES)),
                whole((3, HALF, LANES)),
                whole((2, LANES)),
                whole((6 * LANES, 2 * LANES)),
                whole((TILE, LANES)),
            ],
            out_specs=[whole(out_shape), whole((TILE, LANES))],
            scratch_shapes=[
                pltpu.VMEM((2 * tiles, TILE, 6 * HALF, LANES), jnp.float32),
                pltpu.VMEM((tiles, SEGS * TILE, LANES), jnp.float32),
                pltpu.VMEM((tiles, rows, 4 * LANES), jnp.bfloat16),
                pltpu.VMEM((tiles, SEGS * TILE, LANES), jnp.float32),
                pltpu.VMEM((tiles, rows, 2 * LANES), jnp.float32),
                pltpu.SemaphoreType.DMA((2 * tiles, 3 * TILE)),
            ],
        ),
        out_shape=[
            jax.ShapeDtypeStruct(out_shape, jnp.float32),
            jax.ShapeDtypeStruct((TILE, LANES), jnp.float32),
        ],
        compiler_params=pltpu.CompilerParams(dimension_semantics=("arbitrary",)),
        cost_estimate=pl.CostEstimate(flops=work * COST, transcendentals=0, bytes_accessed=work * SEG * 4),
        name="spectrum",
    )(
        meta,
        by_channel(x),
        by_channel(remote),
        by_channel(halo_a),
        by_channel(halo_b),
        window,
        first_high,
        first_low,
        twiddle,
        edge_twiddle,
        second,
        edges,
    )


def pick_constant():
    table = np.zeros((2, 2 * LANES, LANES), np.float32)
    for q in range(2):
        for k in range(HALF):
            table[q, q * HALF + k, k] = 1.0
            table[q, LANES + q * HALF + k, ROOT - k if k else HALF] = 1.0
    return table


def finish_kernel(tiles, meta, scale_ref, pick_ref, *refs):
    parts, (power_ref, mean_ref, nyquist_ref, band, spread) = refs[:STEPS], refs[STEPS:]
    shard = meta[3]
    for step, part in enumerate(parts):
        for core in range(2):
            for group in range(2):
                span = slice(group * 2 * tiles, (group + 1) * 2 * tiles)
                total = part[core, span]
                for source in range(2 + core, PLACES, 2):
                    total = total + part[source, span]
                first = (core * SIDE + group * (SIDE // 2) + tiles * step) * 2 * TILE
                band[first : first + 2 * tiles * TILE] = total.reshape(2 * tiles * TILE, LANES)
    scale = scale_ref[0]
    lane = lax.broadcasted_iota(jnp.int32, (1, LANES), 1)
    sums = []
    for k in range(2):
        count = band.shape[0] // 4
        lo = band[pl.ds(2 * k, count, stride=4), :]
        hi = band[pl.ds(2 * k + 1, count, stride=4), :]
        both = jnp.concatenate([lo, hi], axis=1)
        first = (lane == 0) & (shard == 0) & (k == 0)
        factor = jnp.where(first, scale, 2.0 * scale)
        total = jnp.zeros((1, LANES), jnp.float32)
        for q in range(2):
            value = (
                jnp.dot(both, pick_ref[q], preferred_element_type=jnp.float32, precision=lax.Precision.HIGHEST)
                * factor
            )
            spread[k, pl.ds(q, count, stride=2), :] = value
            total = total + jnp.sum(value, axis=0, keepdims=True)
        power_ref[:, k * LANES : (k + 1) * LANES] = spread[k]
        sums.append(total)
    mean_ref[...] = jnp.concatenate(sums, axis=1)
    for core in range(2):
        total = parts[-1][core, 4 * tiles]
        for source in range(2 + core, PLACES, 2):
            total = total + parts[-1][source, 4 * tiles]
        nyquist_ref[core * SIDE : (core + 1) * SIDE] = (total * scale).T[:SIDE]


def finish(tiles, meta, scale, parts, rows):
    vmem = pl.BlockSpec(memory_space=pltpu.VMEM)
    smem = pl.BlockSpec(memory_space=pltpu.SMEM)
    return pl.pallas_call(
        functools.partial(finish_kernel, tiles),
        in_specs=[smem, smem, vmem] + [vmem] * len(parts),
        out_specs=[vmem, vmem, vmem],
        out_shape=[
            jax.ShapeDtypeStruct((rows, 2 * LANES), jnp.float32),
            jax.ShapeDtypeStruct((1, 2 * LANES), jnp.float32),
            jax.ShapeDtypeStruct((2 * SIDE, TILE), jnp.float32),
        ],
        scratch_shapes=[
            pltpu.VMEM((rows * 2, LANES), jnp.float32),
            pltpu.VMEM((2, rows, LANES), jnp.float32),
        ],
        name="finish",
    )(meta, scale, pick_constant(), *parts)


def per_device(strain):
    rows, width = strain.shape
    count = lax.axis_size("tm")
    me = lax.axis_index("tm")
    row_tiles = rows // TILE
    tiles = SIDE // 2 // STEPS
    segments = width // (SEG // 2) * count - 1
    core = me & 1
    x = strain.reshape(row_tiles, TILE, ROOT, LANES).swapaxes(1, 2).reshape(row_tiles, ROOT * TILE, LANES)
    same = [(i + 2, i) for i in range(0, count - 2, 2)] + [(i, i + 2) for i in range(1, count - 2, 2)]
    cross = [(i, i + 1) for i in range(1, count - 2, 2)] + [(i + 1, i) for i in range(1, count - 2, 2)]
    swap = [(i, i ^ 1) for i in range(count)]

    def part(tile, offset, tile_count, size):
        return lax.dynamic_slice(x, (tile, offset, 0), (tile_count, size, LANES))

    edge_at = core * (HALF * TILE)
    halos = []
    for step in range(STEPS):
        at = step * tiles
        halo_a = lax.ppermute(part(core * SIDE + at, edge_at, tiles, HALF * TILE), "tm", same)
        halo_b = lax.ppermute(
            part((1 - core) * SIDE + SIDE // 2 + at, edge_at, tiles, HALF * TILE), "tm", cross
        )
        halos.append((halo_a, halo_b))
    remote = lax.ppermute(part((1 - core) * SIDE, 0, SIDE, ROOT * TILE), "tm", swap)
    window, energy = window_table()
    scale = (1.0 / (segments * energy)).reshape(1)
    meta = jnp.stack([core, (me < count - 2).astype(jnp.int32), (me > 1).astype(jnp.int32), me]).astype(jnp.int32)
    constants = dft_constants()
    edges = jnp.zeros((TILE, LANES), jnp.float32)
    parts = []
    for step in range(STEPS):
        out, edges = spectrum(
            step * tiles, tiles, step == STEPS - 1, meta, x, remote, *halos[step], window, constants, edges
        )
        parts.append(lax.all_to_all(out, "tm", 0, 0, tiled=True))
    power, band_sum, nyquist = finish(tiles, meta, scale, parts, rows)
    chans = lax.axis_size("chan")
    total = band_sum
    for shift in range(1, chans):
        total = total + lax.ppermute(band_sum, "chan", [(i, (i + shift) % chans) for i in range(chans)])
    mean_power = (total / (rows * chans)).reshape(-1)
    return power, nyquist.reshape(-1), mean_power


def solution(mesh):
    in_specs = (P("chan", "tm"),)
    out_specs = (P("chan", "tm"), P("chan"), P("tm"))
    return jax.shard_map(per_device, mesh=mesh, in_specs=in_specs, out_specs=out_specs, check_vma=False)
```

time: 175 us -> 173 us (0.989)
  waiting for transfers between devices: 37.9 us -> 62 us
  Pallas kernels: 52.3 us -> 42.1 us
  other arithmetic: 13.7 us -> 3.55 us
  starting transfers between devices: 58.8 us -> 48.8 us
  local copies, waits for them, and re-layouts: 9.75 us -> 14.1 us
    ppermute x12 -> x7, waiting for transfers between devices: 2.51 us -> 42.2 us  [the longest x3 42.2 us: per_device(): lax.ppermute(part(core * SIDE + at, edge_at, tiles, HALF * TILE), 'tm', s...]
    all_to_all x4 -> x3, waiting for transfers between devices: 34.3 us -> 17.2 us  [per_device(): parts.append(lax.all_to_all(out, 'tm', 0, 0, tiled=True))]
    ppermute x12 -> x7, starting transfers between devices: 22.7 us -> 6.91 us  [the longest x3 3.88 us: per_device(): lax.ppermute(part(core * SIDE + at, edge_at, tiles, HALF * TILE), 'tm', s...]
    pallas_call x4 -> x3, Pallas kernels: 49 us -> 38.8 us  [spectrum(): pl.pallas_call(functools.partial(spectrum_kernel, tiles, first, last), gr...]
    add x4 -> x0, other arithmetic: 8.7 us -> none  [per_device(): mine = own + lax.ppermute(other, 'tm', swap)]
    dynamic_slice x0 -> x2, local copies, waits for them, and re-layouts: none -> 7.84 us  [part(): return lax.dynamic_slice(x, (tile, offset, 0), (tile_count, size, LANES))]
    all_to_all x4 -> x3, starting transfers between devices: 30.2 us -> 37.3 us  [per_device(): parts.append(lax.all_to_all(out, 'tm', 0, 0, tiled=True))]
    slice x2 -> x0, local copies, waits for them, and re-layouts: 4.74 us -> none  [the longest x1 4.73 us: per_device(): x[12 + first:12 + first + tiles, HALF * TILE:]]
  transfers between devices with their start and end apart: 19 -> 13, of which waited for: 5 -> 6; matrix products, arithmetic and copies ran while one was open for 9% -> 3% of each run, Pallas kernels for 21% -> 15%
where the time goes in v2:
time: 173 us; the launch traced here: 172 us
  waiting for transfers between devices  62 us (36%)
  starting transfers between devices  48.8 us (28%)
  Pallas kernels  42.1 us (24%)
  local copies, waits for them, and re-layouts  14.1 us (8%)
  other arithmetic  3.55 us (2%)
    ppermute x3, waiting for transfers between devices, per_device(): lax.ppermute(part(core * SIDE + at, edge_at, tiles, HALF * TILE), 'tm', s...  42.2 us
    pallas_call x3, Pallas kernels, spectrum(): pl.pallas_call(functools.partial(spectrum_kernel, tiles, first, last), gr...  38.8 us
    all_to_all x3, starting transfers between devices, per_device(): parts.append(lax.all_to_all(out, 'tm', 0, 0, tiled=True))  37.3 us
    all_to_all x3, waiting for transfers between devices, per_device(): parts.append(lax.all_to_all(out, 'tm', 0, 0, tiled=True))  17.2 us
    dynamic_slice x2, local copies, waits for them, and re-layouts, part(): return lax.dynamic_slice(x, (tile, offset, 0), (tile_count, size, LANES))  7.84 us
    ppermute x3, starting transfers between devices, per_device(): lax.ppermute(band_sum, 'chan', [(i, (i + shift) % chans) for i in range(c...  4.61 us
    unnamed x14, local copies, waits for them, and re-layouts  4.27 us
    ppermute x3, starting transfers between devices, per_device(): lax.ppermute(part(core * SIDE + at, edge_at, tiles, HALF * TILE), 'tm', s...  3.88 us
  transfers between devices with their start and end apart: 13, of which 6 were waited for; matrix products, arithmetic and copies ran while one was open for 3% of the time, Pallas kernels for 15%

profile of v2, /device:TPU:0, one launch (start us, length us, event | category | flops | bytes accessed | tf_op | source)
XLA Modules:
  0.0 172.1 jit_solution(12511549006974053905)
XLA Ops:
  0.6 5.8 %constant_dynamic-slice_fusion.6 = f32[12,1024,128]{2,1,0:T(8,128)} fusion(f32[24,1024,128]{2,1,0:T(8,128)} %bitcast.20, s32[]{:T(128)S(6)} %select_n.29), kind=kLoop, calls=%fused_computation.8 | loop fusion | bytes 12582916 | tf_op jit(solution)/shard_map/dynamic_slice | solution.py:379
  6.4 2.0 %constant_dynamic-slice_fusion = (f32[2,512,128]{2,1,0:T(8,128)S(1)}, f32[2,512,128]{2,1,0:T(8,128)S(1)}, f32[2,512,128]{2,1,0:T(8,128)S(1)}, f32[2,512,128]{2,1...) fusion(f32[24,1024,128]{2,1,0:T(8,128)} %bitcast.21, s32[]{:T(128)S(6)} %select_n.36, ...), kind=kLoop, calls=%fused_computation.2 | loop fusion | bytes 6291484 | tf_op jit(solution)/shard_map/dynamic_slice | solution.py:379
  8.5 1.3 collective-permute-start.1
  9.8 1.5 collective-permute-start.2
  11.8 0.9 multiply_subtract_fusion.window_ref
  12.7 7.0 %collective-permute-done.1 = f32[2,512,128]{2,1,0:T(8,128)} collective-permute-done((f32[2,512,128]{2,1,0:T(8,128)S(1)}, f32[2,512,128]{2,1,0:T(8,128)}, u32[]{:S(2)}, u32[]{:S(2)}) %collective-permute-start.1) | collective-permute-done | bytes 524320 | tf_op jit(solution)/shard_map/ppermute | solution.py:385
  20.3 12.9 %spectrum.3 = (f32[32,8,8,128]{3,2,1,0:T(8,128)}, f32[8,128]{1,0:T(8,128)}) custom-call(s32[4]{0:T(128)} %pad_add_fusion.meta, f32[24,128,8,1,128]{4,3,2,1,0:T(1,128)} %bitcast.22, f32[12,128,8,1,128]{4,3,2,1,0:T(1,128)} %bitcast.10.remote_hbm, f32[2,64,8,1,128]{4,3,2,1,0:T(1,128)} %bitcast.12.halo_a_hbm, f32[2,64,8,1,128]{4,3,2,1,0:T(1,128)} %bitcast.13.halo_b_hbm, ...), custom_call_target="tpu_custom_call" | custom-call | flops 536870912 | bytes 8388608 | tf_op jit(solution)/shard_map/spectrum/pallas_call | solution.py:245
  33.2 15.0 %all-to-all-start = ((f32[32,8,8,128]{3,2,1,0:T(8,128)}), f32[32,8,8,128]{3,2,1,0:T(8,128)S(1)}, u32[]{:S(2)}, u32[]{:S(2)}) async-start(f32[32,8,8,128]{3,2,1,0:T(8,128)} %get-tuple-element.11), calls=%async_computation | async-start | bytes 2097152 | tf_op jit(solution)/shard_map/all_to_all | solution.py:401
  48.2 1.3 collective-permute-start.3
  50.2 17.7 %collective-permute-done.3 = f32[2,512,128]{2,1,0:T(8,128)S(1)} collective-permute-done((f32[2,512,128]{2,1,0:T(8,128)S(1)}, f32[2,512,128]{2,1,0:T(8,128)S(1)}, u32[]{:S(2)}, u32[]{:S(2)}) %collective-permute-start.3) | collective-permute-done | bytes 524320 | tf_op jit(solution)/shard_map/ppermute | solution.py:385
  69.5 13.0 %spectrum.4 = (f32[32,8,8,128]{3,2,1,0:T(8,128)}, f32[8,128]{1,0:T(8,128)}) custom-call(s32[4]{0:T(128)} %pad_add_fusion.meta, f32[24,128,8,1,128]{4,3,2,1,0:T(1,128)} %bitcast.23, f32[12,128,8,1,128]{4,3,2,1,0:T(1,128)} %bitcast.10.remote_hbm, f32[2,64,8,1,128]{4,3,2,1,0:T(1,128)} %bitcast.27, f32[2,64,8,1,128]{4,3,2,1,0:T(1,128)} %bitcast.28, ...), custom_call_target="tpu_custom_call" | custom-call | flops 536870912 | bytes 8388608 | tf_op jit(solution)/shard_map/spectrum/pallas_call | solution.py:245
  82.5 11.1 %all-to-all-start.1 = ((f32[32,8,8,128]{3,2,1,0:T(8,128)}), f32[32,8,8,128]{3,2,1,0:T(8,128)S(1)}, u32[]{:S(2)}, u32[]{:S(2)}) async-start(f32[32,8,8,128]{3,2,1,0:T(8,128)} %get-tuple-element.13), calls=%async_computation.1 | async-start | bytes 2097152 | tf_op jit(solution)/shard_map/all_to_all | solution.py:401
  93.7 1.3 collective-permute-start.5
  95.8 17.5 %collective-permute-done.5 = f32[2,512,128]{2,1,0:T(8,128)S(1)} collective-permute-done((f32[2,512,128]{2,1,0:T(8,128)S(1)}, f32[2,512,128]{2,1,0:T(8,128)S(1)}, u32[]{:S(2)}, u32[]{:S(2)}) %collective-permute-start.5) | collective-permute-done | bytes 524320 | tf_op jit(solution)/shard_map/ppermute | solution.py:385
  115.0 13.0 %spectrum.5 = (f32[32,9,8,128]{3,2,1,0:T(8,128)}, f32[8,128]{1,0:T(8,128)}) custom-call(s32[4]{0:T(128)} %pad_add_fusion.meta, f32[24,128,8,1,128]{4,3,2,1,0:T(1,128)} %bitcast.24, f32[12,128,8,1,128]{4,3,2,1,0:T(1,128)} %bitcast.10.remote_hbm, f32[2,64,8,1,128]{4,3,2,1,0:T(1,128)} %bitcast.25, f32[2,64,8,1,128]{4,3,2,1,0:T(1,128)} %bitcast.26, ...), custom_call_target="tpu_custom_call" | custom-call | flops 536870912 | bytes 8388608 | tf_op jit(solution)/shard_map/spectrum/pallas_call | solution.py:245
  128.0 11.1 %all-to-all-start.2 = ((f32[32,9,8,128]{3,2,1,0:T(8,128)}), f32[32,9,8,128]{3,2,1,0:T(8,128)S(1)}, u32[]{:S(2)}, u32[]{:S(2)}) async-start(f32[32,9,8,128]{3,2,1,0:T(8,128)} %get-tuple-element.15), calls=%async_computation.2 | async-start | bytes 2359296 | tf_op jit(solution)/shard_map/all_to_all | solution.py:401
  140.7 17.2 %all-to-all-done.2.refs_2_ = f32[32,9,8,128]{3,2,1,0:T(8,128)S(1)} async-done(((f32[32,9,8,128]{3,2,1,0:T(8,128)}), f32[32,9,8,128]{3,2,1,0:T(8,128)S(1)}, u32[]{:S(2)}, u32[]{:S(2)}) %all-to-all-start.2) | async-done | bytes 1179680 | tf_op jit(solution)/shard_map/all_to_all | solution.py:401
  157.8 1.0 copy-done
  158.8 3.3 %finish.1 = (f32[192,256]{1,0:T(8,128)}, f32[1,256]{1,0:T(1,128)}, f32[24,8]{1,0:T(8,128)}) custom-call(s32[4]{0:T(128)} %pad_add_fusion.meta, f32[1]{0:T(128)} %bitcast.4.scale_ref, f32[2,256,128]{2,1,0:T(8,128)} %constant.74.clone.pick_ref, f32[32,8,8,128]{3,2,1,0:T(8,128)} %copy-done.1, f32[32,8,8,128]{3,2,1,0:T(8,128)} %copy-done.2, ...), custom_call_target="tpu_custom_call" | custom-call | tf_op jit(solution)/shard_map/finish/pallas_call | solution.py:348
  162.2 3.0 %collective-permute-start.9 = (f32[1,256]{1,0:T(1,128)}, f32[1,256]{1,0:T(1,128)S(1)}, u32[]{:S(2)}, u32[]{:S(2)}) collective-permute-start(f32[1,256]{1,0:T(1,128)} %get-tuple-element.18), channel_id=1, source_target_pairs={{0,96},{32,0},{64,32},{96,64},{1,97},{33,1},{65,33},{97,65},{2,98}... | collective-permute-start | bytes 3080 | tf_op jit(solution)/shard_map/ppermute | solution.py:406
  165.8 1.0 collective-permute-start.7
  166.8 1.4 reshape.56
  168.1 2.3 %collective-permute-done.8 = f32[1,256]{1,0:T(1,128)S(1)} collective-permute-done((f32[1,256]{1,0:T(1,128)}, f32[1,256]{1,0:T(1,128)S(1)}, u32[]{:S(2)}, u32[]{:S(2)}) %collective-permute-start.8) | collective-permute-done | bytes 1056 | tf_op jit(solution)/shard_map/ppermute | solution.py:406
  170.8 1.2 add_multiply_fusion
  (28 shorter events, 7.8 us)
Async XLA Ops:
  6.4 13.2 %collective-permute-start = (f32[12,1024,128]{2,1,0:T(8,128)}, f32[12,1024,128]{2,1,0:T(8,128)}, u32[]{:S(2)}, u32[]{:S(2)}) collective-permute-start(f32[12,1024,128]{2,1,0:T(8,128)} %constant_dynamic-slice_fusion.6), channel_id=1, source_target_pairs={{0,1},{1,0},{2,3},{3,2},{4,5},{5,4},{6,7},{7,6},{8,9},{9,8},{10,11... | collective-permute-start | bytes 18874376 | tf_op jit(solution)/shard_map/ppermute | solution.py:390
  8.5 11.2 %collective-permute-start.1 = (f32[2,512,128]{2,1,0:T(8,128)S(1)}, f32[2,512,128]{2,1,0:T(8,128)}, u32[]{:S(2)}, u32[]{:S(2)}) collective-permute-start(f32[2,512,128]{2,1,0:T(8,128)S(1)} %get-tuple-element.24), channel_id=1, source_target_pairs={{2,0},{4,2},{6,4},{8,6},{10,8},{12,10},{14,12},{16,14},{18,16},{20... | collective-permute-start | bytes 1572872 | tf_op jit(solution)/shard_map/ppermute | solution.py:385
  9.8 9.9 %collective-permute-start.2 = (f32[2,512,128]{2,1,0:T(8,128)S(1)}, f32[2,512,128]{2,1,0:T(8,128)}, u32[]{:S(2)}, u32[]{:S(2)}) collective-permute-start(f32[2,512,128]{2,1,0:T(8,128)S(1)} %get-tuple-element.23), channel_id=1, source_target_pairs={{1,2},{3,4},{5,6},{7,8},{9,10},{11,12},{13,14},{15,16},{17,18},{19... | collective-permute-start | bytes 1572872 | tf_op jit(solution)/shard_map/ppermute | solution.py:386
  33.2 49.3 %all-to-all-start = ((f32[32,8,8,128]{3,2,1,0:T(8,128)}), f32[32,8,8,128]{3,2,1,0:T(8,128)S(1)}, u32[]{:S(2)}, u32[]{:S(2)}) async-start(f32[32,8,8,128]{3,2,1,0:T(8,128)} %get-tuple-element.11), calls=%async_computation | async-start | bytes 2097152 | tf_op jit(solution)/shard_map/all_to_all | solution.py:401
  48.2 19.7 %collective-permute-start.3 = (f32[2,512,128]{2,1,0:T(8,128)S(1)}, f32[2,512,128]{2,1,0:T(8,128)S(1)}, u32[]{:S(2)}, u32[]{:S(2)}) collective-permute-start(f32[2,512,128]{2,1,0:T(8,128)S(1)} %get-tuple-element.22), channel_id=1, source_target_pairs={{2,0},{4,2},{6,4},{8,6},{10,8},{12,10},{14,12},{16,14},{18,16},{20... | collective-permute-start | bytes 1572872 | tf_op jit(solution)/shard_map/ppermute | solution.py:385
  49.5 18.4 %collective-permute-start.4 = (f32[2,512,128]{2,1,0:T(8,128)S(1)}, f32[2,512,128]{2,1,0:T(8,128)S(1)}, u32[]{:S(2)}, u32[]{:S(2)}) collective-permute-start(f32[2,512,128]{2,1,0:T(8,128)S(1)} %get-tuple-element.21), channel_id=1, source_target_pairs={{1,2},{3,4},{5,6},{7,8},{9,10},{11,12},{13,14},{15,16},{17,18},{19... | collective-permute-start | bytes 1572872 | tf_op jit(solution)/shard_map/ppermute | solution.py:386
  67.9 0.8 copy-start.5
  68.7 0.9 copy-start.6
  82.5 45.4 %copy-start.1 = (f32[32,8,8,128]{3,2,1,0:T(8,128)}, f32[32,8,8,128]{3,2,1,0:T(8,128)S(1)}, u32[]{:S(2)}) copy-start(f32[32,8,8,128]{3,2,1,0:T(8,128)S(1)} %all-to-all-done.refs_0_) | copy-start | bytes 3145732
  82.5 45.4 %all-to-all-start.1 = ((f32[32,8,8,128]{3,2,1,0:T(8,128)}), f32[32,8,8,128]{3,2,1,0:T(8,128)S(1)}, u32[]{:S(2)}, u32[]{:S(2)}) async-start(f32[32,8,8,128]{3,2,1,0:T(8,128)} %get-tuple-element.13), calls=%async_computation.1 | async-start | bytes 2097152 | tf_op jit(solution)/shard_map/all_to_all | solution.py:401
  93.7 19.7 %collective-permute-start.5 = (f32[2,512,128]{2,1,0:T(8,128)S(1)}, f32[2,512,128]{2,1,0:T(8,128)S(1)}, u32[]{:S(2)}, u32[]{:S(2)}) collective-permute-start(f32[2,512,128]{2,1,0:T(8,128)S(1)} %get-tuple-element.20), channel_id=1, source_target_pairs={{2,0},{4,2},{6,4},{8,6},{10,8},{12,10},{14,12},{16,14},{18,16},{20... | collective-permute-start | bytes 1572872 | tf_op jit(solution)/shard_map/ppermute | solution.py:385
  95.0 18.4 %collective-permute-start.6 = (f32[2,512,128]{2,1,0:T(8,128)S(1)}, f32[2,512,128]{2,1,0:T(8,128)S(1)}, u32[]{:S(2)}, u32[]{:S(2)}) collective-permute-start(f32[2,512,128]{2,1,0:T(8,128)S(1)} %get-tuple-element.19), channel_id=1, source_target_pairs={{1,2},{3,4},{5,6},{7,8},{9,10},{11,12},{13,14},{15,16},{17,18},{19... | collective-permute-start | bytes 1572872 | tf_op jit(solution)/shard_map/ppermute | solution.py:386
  113.4 0.8 copy-start.3
  114.1 0.8 copy-start.4
  128.0 29.8 %copy-start.2 = (f32[32,8,8,128]{3,2,1,0:T(8,128)}, f32[32,8,8,128]{3,2,1,0:T(8,128)S(1)}, u32[]{:S(2)}) copy-start(f32[32,8,8,128]{3,2,1,0:T(8,128)S(1)} %all-to-all-done.1.refs_1_) | copy-start | bytes 3145732
  128.0 29.8 %all-to-all-start.2 = ((f32[32,9,8,128]{3,2,1,0:T(8,128)}), f32[32,9,8,128]{3,2,1,0:T(8,128)S(1)}, u32[]{:S(2)}, u32[]{:S(2)}) async-start(f32[32,9,8,128]{3,2,1,0:T(8,128)} %get-tuple-element.15), calls=%async_computation.2 | async-start | bytes 2359296 | tf_op jit(solution)/shard_map/all_to_all | solution.py:401
  157.8 1.0 copy-start
  162.2 6.0 %collective-permute-start.9 = (f32[1,256]{1,0:T(1,128)}, f32[1,256]{1,0:T(1,128)S(1)}, u32[]{:S(2)}, u32[]{:S(2)}) collective-permute-start(f32[1,256]{1,0:T(1,128)} %get-tuple-element.18), channel_id=1, source_target_pairs={{0,96},{32,0},{64,32},{96,64},{1,97},{33,1},{65,33},{97,65},{2,98}... | collective-permute-start | bytes 3080 | tf_op jit(solution)/shard_map/ppermute | solution.py:406
  165.2 5.3 %collective-permute-start.8 = (f32[1,256]{1,0:T(1,128)}, f32[1,256]{1,0:T(1,128)S(1)}, u32[]{:S(2)}, u32[]{:S(2)}) collective-permute-start(f32[1,256]{1,0:T(1,128)} %get-tuple-element.18), channel_id=1, source_target_pairs={{0,64},{32,96},{64,0},{96,32},{1,65},{33,97},{65,1},{97,33},{2,66}... | collective-permute-start | bytes 3080 | tf_op jit(solution)/shard_map/ppermute | solution.py:406
  165.8 5.0 %collective-permute-start.7 = (f32[1,256]{1,0:T(1,128)}, f32[1,256]{1,0:T(1,128)S(1)}, u32[]{:S(2)}, u32[]{:S(2)}) collective-permute-start(f32[1,256]{1,0:T(1,128)} %get-tuple-element.18), channel_id=1, source_target_pairs={{0,32},{32,64},{64,96},{96,0},{1,33},{33,65},{65,97},{97,1},{2,34}... | collective-permute-start | bytes 3080 | tf_op jit(solution)/shard_map/ppermute | solution.py:406

commit v3 on v2

v3 whole, which is shorter than its diff:
```python
import functools

import jax
import jax.numpy as jnp
import numpy as np
from jax import lax
from jax.experimental import pallas as pl
from jax.experimental.pallas import tpu as pltpu
from jax.sharding import PartitionSpec as P


SEG = 16384
ROOT = 128
HALF = ROOT // 2
TILE = 8
LANES = 128
CHUNKS = (4, 8)
STEPS = len(CHUNKS)
SIDE = 12
PLACES = 32
SEGS = 4
COST = 1 << 22


def split_bf16(table):
    high = table.astype(jnp.bfloat16)
    low = (table - high.astype(np.float64)).astype(jnp.bfloat16)
    return high, low


def dft_constants():
    n = np.arange(ROOT)
    angle = 2.0 * np.pi * ((n[:, None] * n[None, :]) % ROOT) / ROOT
    rows = np.arange(HALF)
    first = np.concatenate([np.cos(angle[:HALF]), -np.sin(angle[:HALF])], axis=0)
    first[HALF] = 1.0 - 2.0 * (n % 2)
    high, low = split_bf16(first)
    first_high = np.concatenate([high, high], axis=1)
    twist = 2.0 * np.pi * (rows[:, None] * n[None, :]) / SEG
    cos_twist = np.cos(twist)
    cos_imag = cos_twist.copy()
    cos_imag[0] = 0.0
    twiddle = np.stack([cos_twist, cos_imag, np.sin(twist)]).astype(np.float32)
    edge = np.pi * n / ROOT
    edge_twiddle = np.stack([np.cos(edge), -np.sin(edge)]).astype(np.float32)
    columns = []
    for k in range(HALF):
        columns += [k, ROOT - 1 - k]
    c = np.cos(angle[:, columns])
    s = np.sin(angle[:, columns])
    high, low_second = split_bf16(np.block([[c, -s], [s, c]]))
    second = np.concatenate([high, high, low_second], axis=0)
    window = (0.5 - 0.5 * np.cos(2.0 * np.pi * np.arange(SEG) / SEG)).astype(np.float32)
    reals = np.concatenate([window.reshape(ROOT, LANES), *twiddle, edge_twiddle, np.zeros((6, LANES), np.float32)])
    left = np.concatenate([first_high, low], axis=1)
    return reals, left, second, float(np.sum(window.astype(np.float64) ** 2))


def spectrum_kernel(
    tiles,
    first,
    skip,
    last,
    x_hbm,
    remote_hbm,
    halo_hbm,
    reals_ref,
    first_ref,
    second_ref,
    edges_in_ref,
    out_ref,
    edges_ref,
    x_buf,
    means,
    spec,
    corner,
    result,
    sems,
):
    step = pl.program_id(0)
    me = lax.axis_index("tm")
    core = me & 1
    right = 1 - core
    near = pl.multiple_of(HALF + ROOT * core, HALF)
    far = pl.multiple_of(HALF + ROOT * right, HALF)
    outer_at = pl.multiple_of(right * (5 * HALF), HALF)
    outer_start = pl.multiple_of(right * (4 * HALF), HALF)
    starts = (HALF, 2 * HALF, 3 * HALF, outer_start)
    inside = jnp.where(right == 1, me < lax.axis_size("tm") - 2, me > 1)
    keep = jnp.where(inside, 1.0, 0.0).astype(jnp.float32)
    base = step

    @pl.when(step == 0)
    def _():
        for u in range(tiles):
            for c in range(TILE):
                for src, at, size in (
                    (x_hbm.at[core * SIDE + first + u, :, c, 0, :], near, ROOT),
                    (remote_hbm.at[skip + u, :, c, 0, :], far, ROOT),
                    (halo_hbm.at[skip + u, :, c, 0, :], outer_at, HALF),
                ):
                    pltpu.make_async_copy(src, x_buf.at[u, c, pl.ds(at, size), :], sems.at[u]).start()
        edges_ref[...] = edges_in_ref[...] if first else jnp.zeros((TILE, LANES), jnp.float32)

    def wait_for(u):
        whole = x_buf.at[base + u, :, pl.ds(0, 5 * HALF), :]
        pltpu.make_async_copy(whole, whole, sems.at[base + u]).wait()

    def average(u):
        def part(c, at):
            return jnp.sum(x_buf[base + u, c, pl.ds(at, HALF), :].reshape(HALF // TILE, TILE, LANES), axis=0)

        sums = [[] for _ in range(SEGS)]
        for c in range(TILE):
            q = [part(c, HALF * (k + 1)) for k in range(4)]
            outer = part(c, outer_at) + jnp.where(right == 1, q[3], q[0])
            for k, value in enumerate((q[0] + q[1], q[1] + q[2], q[2] + q[3], outer)):
                sums[k].append(value)
        both = jnp.stack(sum(sums, []))
        total = jnp.sum(jnp.sum(both, axis=1), axis=1, keepdims=True) * (1.0 / SEG)
        means[...] = jnp.broadcast_to(total, (SEGS * TILE, LANES))

    def put(pair, row, size, part, value):
        high = value.astype(jnp.bfloat16)
        lanes = slice(part * LANES, (part + 1) * LANES)
        lanes_low = slice((2 + part) * LANES, (3 + part) * LANES)
        spec[pair, row : row + size, lanes] = high
        spec[pair, row : row + size, lanes_low] = (value - high.astype(jnp.float32)).astype(jnp.bfloat16)

    rows = 2 * SEGS * HALF

    def forward(pair):
        for seg in range(SEGS):
            highs = []
            lows = []
            for q in range(2):
                c = 2 * pair + q
                r = seg * TILE + c
                piece = x_buf[step, c, pl.ds(starts[seg], ROOT), :]
                centred = (piece - means[r : r + 1, :]) * reals_ref[:ROOT]
                high = centred.astype(jnp.bfloat16)
                highs.append(high)
                lows.append((centred - high.astype(jnp.float32)).astype(jnp.bfloat16))
            high = jnp.concatenate(highs, axis=1)
            low = jnp.concatenate(lows, axis=1)
            stage = jnp.dot(
                first_ref[...], jnp.concatenate([high, low, high], axis=0), preferred_element_type=jnp.float32
            )
            for q in range(2):
                real = stage[:HALF, q * LANES : (q + 1) * LANES]
                imag = stage[HALF:, q * LANES : (q + 1) * LANES]
                r = 2 * seg + q
                corner[pair, r : r + 1, :] = imag[0:1]
                cos_real = reals_ref[ROOT : ROOT + HALF]
                cos_imag = reals_ref[ROOT + HALF : 2 * ROOT]
                sin_both = reals_ref[2 * ROOT : 2 * ROOT + HALF]
                put(pair, r * HALF, HALF, 0, real * cos_real + imag * sin_both)
                put(pair, r * HALF, HALF, 1, imag * cos_imag - real * sin_both)

    def second(pair):
        edge = 2 * ROOT + HALF
        for part in range(2):
            put(pair, rows, TILE, part, corner[pair] * reals_ref[edge + part : edge + part + 1])
        left = jnp.concatenate([spec[pair], spec[pair, :, : 2 * LANES]], axis=1)
        result[pair] = jnp.dot(left, second_ref[...], preferred_element_type=jnp.float32)

    row_id = lax.broadcasted_iota(jnp.int32, (HALF, LANES), 0)
    lane_id = lax.broadcasted_iota(jnp.int32, (HALF, LANES), 1)
    replaced = (row_id == 0) & (lane_id % 2 == 1)
    tile_lane = lax.broadcasted_iota(jnp.int32, (TILE, LANES), 1)
    tile_row = lax.broadcasted_iota(jnp.int32, (TILE, LANES), 0)
    lower_rows = tile_row < TILE // 2
    edge_rows = []

    def column(pair):
        def power_of(start, size):
            real = result[pair, start : start + size, :LANES]
            imag = result[pair, start : start + size, LANES:]
            return real * real + imag * imag

        edge_power = power_of(rows, TILE)
        blocks = []
        for q in range(2):
            total = keep * power_of((6 + q) * HALF, HALF)
            edge = keep * edge_power[6 + q : 7 + q]
            for seg in range(3):
                total = total + power_of((2 * seg + q) * HALF, HALF)
                edge = edge + edge_power[2 * seg + q : 2 * seg + q + 1]
            edge_rows.append(total[0:1])
            blocks.append(jnp.where(replaced, edge, total))
        return jnp.concatenate(blocks, axis=0).T

    def store(half, a, b):
        at = 2 * step + half
        for place in range(PLACES // 2):
            va = a[place * TILE : (place + 1) * TILE]
            vb = b[place * TILE : (place + 1) * TILE]
            out_ref[2 * place, at] = jnp.where(lower_rows, va, pltpu.roll(vb, 4, 0))
            out_ref[2 * place + 1, at] = jnp.where(lower_rows, pltpu.roll(va, 4, 0), vb)

    wait_for(0)
    average(0)
    forward(0)
    second(0)
    forward(1)
    second(1)
    first_column = column(0)
    forward(2)
    second(2)
    store(0, first_column, column(1))
    forward(3)
    second(3)
    first_column = column(2)
    store(1, first_column, column(3))
    edge_tile = jnp.zeros((TILE, LANES), jnp.float32)
    for c, row in enumerate(edge_rows):
        edge_tile = jnp.where(tile_row == c, row, edge_tile)
    edge_value = jnp.sum(jnp.where(tile_lane == LANES - 1, edge_tile, 0.0), axis=1, keepdims=True)
    edges_ref[...] = jnp.where(tile_lane == first + step, edge_value, edges_ref[...])
    if last:

        @pl.when(step == tiles - 1)
        def _():
            for place in range(PLACES):
                out_ref[place, 2 * tiles] = edges_ref[...]


def spectrum(first, tiles, skip, last, x, remote, halo, constants, edges):
    reals, left, second, _ = constants
    whole = lambda shape: pl.BlockSpec(shape, lambda i: (0,) * len(shape))
    hbm = pl.BlockSpec(memory_space=pl.ANY)
    out_shape = (PLACES, 2 * tiles + int(last), TILE, LANES)
    rows = 2 * SEGS * HALF + TILE
    by_channel = lambda v: v.reshape(-1, v.shape[1] // TILE, TILE, 1, LANES)
    work = tiles * SEGS * TILE
    return pl.pallas_call(
        functools.partial(spectrum_kernel, tiles, first, skip, last),
        grid_spec=pltpu.PrefetchScalarGridSpec(
            num_scalar_prefetch=0,
            grid=(tiles,),
            in_specs=[
                hbm,
                hbm,
                hbm,
                whole(reals.shape),
                whole(left.shape),
                whole(second.shape),
                whole((TILE, LANES)),
            ],
            out_specs=[whole(out_shape), whole((TILE, LANES))],
            scratch_shapes=[
                pltpu.VMEM((tiles, TILE, 6 * HALF, LANES), jnp.float32),
                pltpu.VMEM((SEGS * TILE, LANES), jnp.float32),
                pltpu.VMEM((TILE // 2, rows, 4 * LANES), jnp.bfloat16),
                pltpu.VMEM((TILE // 2, TILE, LANES), jnp.float32),
                pltpu.VMEM((TILE // 2, rows, 2 * LANES), jnp.float32),
                pltpu.SemaphoreType.DMA((tiles,)),
            ],
        ),
        out_shape=[
            jax.ShapeDtypeStruct(out_shape, jnp.float32),
            jax.ShapeDtypeStruct((TILE, LANES), jnp.float32),
        ],
        compiler_params=pltpu.CompilerParams(dimension_semantics=("arbitrary",)),
        cost_estimate=pl.CostEstimate(flops=work * COST, transcendentals=0, bytes_accessed=work * SEG * 4),
        name="spectrum",
    )(
        by_channel(x),
        by_channel(remote),
        by_channel(halo),
        reals,
        left,
        second,
        edges,
    )


def gather_kernel(tiles, first, x_hbm, halo_out, swap_out, halo_buf, swap_buf, sems):
    core = lax.axis_index("tm") & 1
    mine = core * SIDE + first
    theirs = (1 - core) * SIDE + first
    edge = pl.multiple_of(core * (HALF * TILE), HALF * TILE)
    loads = []
    stores = []
    for u in range(tiles):
        source = x_hbm.at[mine + u, pl.ds(edge, HALF * TILE), :]
        loads.append(pltpu.make_async_copy(source, halo_buf.at[u], sems.at[0, u]))
        stores.append(pltpu.make_async_copy(halo_buf.at[u], halo_out.at[u], sems.at[1, u]))
    for u in range(tiles):
        loads.append(pltpu.make_async_copy(x_hbm.at[theirs + u], swap_buf.at[u], sems.at[0, tiles + u]))
        stores.append(pltpu.make_async_copy(swap_buf.at[u], swap_out.at[u], sems.at[1, tiles + u]))
    for copy in loads:
        copy.start()
    for load, store in zip(loads, stores):
        load.wait()
        store.start()
    for copy in stores:
        copy.wait()


def gather(tiles, first, x):
    hbm = pl.BlockSpec(memory_space=pl.ANY)
    return pl.pallas_call(
        functools.partial(gather_kernel, tiles, first),
        in_specs=[hbm],
        out_specs=[hbm, hbm],
        out_shape=[
            jax.ShapeDtypeStruct((tiles, HALF * TILE, LANES), jnp.float32),
            jax.ShapeDtypeStruct((tiles, ROOT * TILE, LANES), jnp.float32),
        ],
        scratch_shapes=[
            pltpu.VMEM((tiles, HALF * TILE, LANES), jnp.float32),
            pltpu.VMEM((tiles, ROOT * TILE, LANES), jnp.float32),
            pltpu.SemaphoreType.DMA((2, 2 * tiles)),
        ],
        name="gather",
    )(x)


def pick_constant():
    table = np.zeros((2, 2 * LANES, LANES), np.float32)
    for q in range(2):
        for k in range(HALF):
            table[q, q * HALF + k, k] = 1.0
            table[q, LANES + q * HALF + k, ROOT - k if k else HALF] = 1.0
    return table


def finish_kernel(scale_ref, pick_ref, *refs):
    parts, (power_ref, mean_ref, nyquist_ref, band, spread) = refs[:STEPS], refs[STEPS:]
    shard = lax.axis_index("tm")
    done = 0
    for tiles, part in zip(CHUNKS, parts):
        for core in range(2):
            total = part[core, : 2 * tiles]
            for source in range(2 + core, PLACES, 2):
                total = total + part[source, : 2 * tiles]
            first = (core * SIDE + done) * 2 * TILE
            band[first : first + 2 * tiles * TILE] = total.reshape(2 * tiles * TILE, LANES)
        done += tiles
    scale = scale_ref[0]
    lane = lax.broadcasted_iota(jnp.int32, (1, LANES), 1)
    sums = []
    for k in range(2):
        count = band.shape[0] // 4
        lo = band[pl.ds(2 * k, count, stride=4), :]
        hi = band[pl.ds(2 * k + 1, count, stride=4), :]
        both = jnp.concatenate([lo, hi], axis=1)
        first = (lane == 0) & (shard == 0) & (k == 0)
        factor = jnp.where(first, scale, 2.0 * scale)
        total = jnp.zeros((1, LANES), jnp.float32)
        for q in range(2):
            value = (
                jnp.dot(both, pick_ref[q], preferred_element_type=jnp.float32, precision=lax.Precision.HIGHEST)
                * factor
            )
            spread[k, pl.ds(q, count, stride=2), :] = value
            total = total + jnp.sum(value, axis=0, keepdims=True)
        power_ref[:, k * LANES : (k + 1) * LANES] = spread[k]
        sums.append(total)
    mean_ref[...] = jnp.concatenate(sums, axis=1)
    for core in range(2):
        total = parts[-1][core, 2 * CHUNKS[-1]]
        for source in range(2 + core, PLACES, 2):
            total = total + parts[-1][source, 2 * CHUNKS[-1]]
        nyquist_ref[core * SIDE : (core + 1) * SIDE] = (total * scale).T[:SIDE]


def finish(scale, parts, rows):
    vmem = pl.BlockSpec(memory_space=pltpu.VMEM)
    smem = pl.BlockSpec(memory_space=pltpu.SMEM)
    return pl.pallas_call(
        finish_kernel,
        in_specs=[smem, vmem] + [vmem] * len(parts),
        out_specs=[vmem, vmem, vmem],
        out_shape=[
            jax.ShapeDtypeStruct((rows, 2 * LANES), jnp.float32),
            jax.ShapeDtypeStruct((1, 2 * LANES), jnp.float32),
            jax.ShapeDtypeStruct((2 * SIDE, TILE), jnp.float32),
        ],
        scratch_shapes=[
            pltpu.VMEM((rows * 2, LANES), jnp.float32),
            pltpu.VMEM((2, rows, LANES), jnp.float32),
        ],
        name="finish",
    )(scale, pick_constant(), *parts)


def per_device(strain):
    rows, width = strain.shape
    count = lax.axis_size("tm")
    row_tiles = rows // TILE
    segments = width // (SEG // 2) * count - 1
    x = strain.reshape(row_tiles, TILE, ROOT, LANES).swapaxes(1, 2).reshape(row_tiles, ROOT * TILE, LANES)
    same = [(i + 2, i) for i in range(0, count - 2, 2)] + [(i, i + 2) for i in range(1, count - 2, 2)]
    swap = [(i, i ^ 1) for i in range(count)]

    moved = []
    for at, tiles in ((0, CHUNKS[0]), (CHUNKS[0], SIDE - CHUNKS[0])):
        edge, other = gather(tiles, at, x)
        halo = lax.ppermute(edge, "tm", same)
        remote = lax.ppermute(other, "tm", swap)
        moved.append((remote, halo))
    constants = dft_constants()
    scale = jnp.full((1,), 1.0 / (segments * constants[3]), jnp.float32)
    edges = np.zeros((TILE, LANES), np.float32)
    parts = []
    done = 0
    for step, tiles in enumerate(CHUNKS):
        out, edges = spectrum(
            done,
            tiles,
            done - CHUNKS[0] if step else 0,
            step == STEPS - 1,
            x,
            *moved[min(step, 1)],
            constants,
            edges,
        )
        parts.append(lax.all_to_all(out, "tm", 0, 0, tiled=True))
        done += tiles
    power, band_sum, nyquist = finish(scale, parts, rows)
    chans = lax.axis_size("chan")
    total = band_sum
    for shift in range(1, chans):
        total = total + lax.ppermute(band_sum, "chan", [(i, (i + shift) % chans) for i in range(chans)])
    mean_power = (total / (rows * chans)).reshape(-1)
    return power, nyquist.reshape(-1), mean_power


def solution(mesh):
    in_specs = (P("chan", "tm"),)
    out_specs = (P("chan", "tm"), P("chan"), P("tm"))
    return jax.shard_map(per_device, mesh=mesh, in_specs=in_specs, out_specs=out_specs, check_vma=False)
```

time: 173 us -> 145 us (0.84)
  blocking collectives: 0 us -> 37.7 us
  starting transfers between devices: 48.8 us -> 17.8 us
  waiting for transfers between devices: 62 us -> 39.4 us
  local copies, waits for them, and re-layouts: 14.1 us -> 3.69 us
  other arithmetic: 3.55 us -> 1.25 us
    all_to_all x0 -> x1, blocking collectives: none -> 37.7 us  [per_device(): parts.append(lax.all_to_all(out, 'tm', 0, 0, tiled=True))]
    all_to_all x3 -> x1, starting transfers between devices: 37.3 us -> 9.98 us  [per_device(): parts.append(lax.all_to_all(out, 'tm', 0, 0, tiled=True))]
    all_to_all x3 -> x1, waiting for transfers between devices: 17.2 us -> 0.01 us  [per_device(): parts.append(lax.all_to_all(out, 'tm', 0, 0, tiled=True))]
    dynamic_slice x2 -> x0, local copies, waits for them, and re-layouts: 7.84 us -> none  [part(): return lax.dynamic_slice(x, (tile, offset, 0), (tile_count, size, LANES))]
    ppermute x7 -> x4, waiting for transfers between devices: 42.2 us -> 36.8 us  [the longest x2 36.8 us: per_device(): halo = lax.ppermute(edge, 'tm', same)]
    ppermute x7 -> x4, starting transfers between devices: 6.91 us -> 3.22 us  [the longest x2 2.57 us: per_device(): halo = lax.ppermute(edge, 'tm', same)]
    unnamed x14 -> x6, local copies, waits for them, and re-layouts: 4.27 us -> 1.69 us
    pallas_call x4 -> x5, Pallas kernels: 42.1 us -> 43.6 us  [the longest x2 32 us: spectrum(): pl.pallas_call(functools.partial(spectrum_kernel, tiles, first, skip, las...]
  transfers between devices with their start and end apart: 13 -> 8, of which waited for: 6 -> 3; matrix products, arithmetic and copies ran while one was open for 3% -> 1% of each run, Pallas kernels for 15% -> 24%
where the time goes in v3:
time: 145 us; the launch traced here: 144 us
  Pallas kernels  43.6 us (30%)
  waiting for transfers between devices  39.4 us (27%)
  blocking collectives  37.7 us (26%)
  starting transfers between devices  17.8 us (12%)
  local copies, waits for them, and re-layouts  3.69 us (3%)
    all_to_all x1, blocking collectives, per_device(): parts.append(lax.all_to_all(out, 'tm', 0, 0, tiled=True))  37.7 us
    ppermute x2, waiting for transfers between devices, per_device(): halo = lax.ppermute(edge, 'tm', same)  36.8 us
    pallas_call x2, Pallas kernels, spectrum(): pl.pallas_call(functools.partial(spectrum_kernel, tiles, first, skip, las...  32 us
    all_to_all x1, starting transfers between devices, per_device(): parts.append(lax.all_to_all(out, 'tm', 0, 0, tiled=True))  9.98 us
    pallas_call x2, Pallas kernels, gather(): pl.pallas_call(functools.partial(gather_kernel, tiles, first), in_specs=[...  8.32 us
    ppermute x3, starting transfers between devices, per_device(): lax.ppermute(band_sum, 'chan', [(i, (i + shift) % chans) for i in range(c...  4.61 us
    pallas_call x1, Pallas kernels, finish(): pl.pallas_call(finish_kernel, in_specs=[smem, vmem] + [vmem] * len(parts)...  3.36 us
  transfers between devices with their start and end apart: 8, of which 3 were waited for; matrix products, arithmetic and copies ran while one was open for 1% of the time, Pallas kernels for 24%

profile of v3, /device:TPU:0, one launch (start us, length us, event | category | flops | bytes accessed | tf_op | source)
XLA Modules:
  0.0 144.3 jit_solution(15213635025060370676)
XLA Ops:
  0.6 5.5 %gather.3 = (f32[8,512,128]{2,1,0:T(8,128)}, f32[8,1024,128]{2,1,0:T(8,128)}) custom-call(f32[24,1024,128]{2,1,0:T(8,128)} %bitcast.12), custom_call_target="tpu_custom_call" | custom-call | tf_op jit(solution)/shard_map/gather/pallas_call | solution.py:303
  6.1 0.1 collective-permute-start.2
  6.2 2.9 %gather.2 = (f32[4,512,128]{2,1,0:T(8,128)}, f32[4,1024,128]{2,1,0:T(8,128)}) custom-call(f32[24,1024,128]{2,1,0:T(8,128)} %bitcast.13), custom_call_target="tpu_custom_call" | custom-call | tf_op jit(solution)/shard_map/gather/pallas_call | solution.py:303
  9.1 0.6 collective-permute-start
  9.6 1.3 collective-permute-start.3
  10.9 1.3 collective-permute-start.1
  12.2 36.8 %collective-permute-done.1 = f32[4,512,128]{2,1,0:T(8,128)S(1)} collective-permute-done((f32[4,512,128]{2,1,0:T(8,128)}, f32[4,512,128]{2,1,0:T(8,128)S(1)}, u32[]{:S(2)}, u32[]{:S(2)}) %collective-permute-start.1) | collective-permute-done | bytes 1048608 | tf_op jit(solution)/shard_map/ppermute | solution.py:401
  49.0 0.6 jit_solution_.3.edges_in_ref
  49.6 0.3 copy-done.2
  50.0 11.7 %spectrum.2 = (f32[32,8,8,128]{3,2,1,0:T(8,128)}, f32[8,128]{1,0:T(8,128)}) custom-call(f32[24,128,8,1,128]{4,3,2,1,0:T(1,128)} %bitcast.14, f32[4,128,8,1,128]{4,3,2,1,0:T(1,128)} %bitcast.5.remote_hbm, f32[4,64,8,1,128]{4,3,2,1,0:T(1,128)} %bitcast.17, f32[328,128]{1,0:T(8,128)} %constant.15.clone.reals_ref, bf16[128,384]{1,0:T(8,128)(2,1)} %constant.16.clone.first_ref, ...), custom_call_target="tpu_custom_call" | custom-call | flops 536870912 | bytes 8388608 | tf_op jit(solution)/shard_map/spectrum/pallas_call | solution.py:236
  61.7 10.0 %all-to-all-start = ((f32[32,8,8,128]{3,2,1,0:T(8,128)}), f32[32,8,8,128]{3,2,1,0:T(8,128)S(1)}, u32[]{:S(2)}, u32[]{:S(2)}) async-start(f32[32,8,8,128]{3,2,1,0:T(8,128)} %get-tuple-element.15), calls=%async_computation | async-start | bytes 2097152 | tf_op jit(solution)/shard_map/all_to_all | solution.py:420
  71.6 0.0 collective-permute-done.3
  71.7 0.0 collective-permute-done.2
  71.7 1.3 copy-done.1
  73.0 20.3 %spectrum.3 = (f32[32,17,8,128]{3,2,1,0:T(8,128)}, f32[8,128]{1,0:T(8,128)}) custom-call(f32[24,128,8,1,128]{4,3,2,1,0:T(1,128)} %bitcast.15, f32[8,128,8,1,128]{4,3,2,1,0:T(1,128)} %bitcast.9.remote_hbm, f32[8,64,8,1,128]{4,3,2,1,0:T(1,128)} %bitcast.16, f32[328,128]{1,0:T(8,128)} %constant.15.clone.reals_ref, bf16[128,384]{1,0:T(8,128)(2,1)} %constant.16.clone.first_ref, ...), custom_call_target="tpu_custom_call" | custom-call | flops 1073741824 | bytes 16777216 | tf_op jit(solution)/shard_map/spectrum/pallas_call | solution.py:236
  93.3 37.7 %all_to_all.10.refs_1_ = f32[32,17,8,128]{3,2,1,0:T(8,128)} all-to-all(f32[32,17,8,128]{3,2,1,0:T(8,128)} %get-tuple-element.19), channel_id=1, replica_groups=mesh['chan'=4,'tm'=32] {'tm'}, dimensions={0} | all-to-all | bytes 4456448 | tf_op jit(solution)/shard_map/all_to_all | solution.py:420
  131.1 3.4 %finish.1 = (f32[192,256]{1,0:T(8,128)}, f32[1,256]{1,0:T(1,128)}, f32[24,8]{1,0:T(8,128)}) custom-call(f32[1]{0:T(128)} %constant.6.clone.1.scale_ref, f32[2,256,128]{2,1,0:T(8,128)} %constant.19.clone.pick_ref, f32[32,8,8,128]{3,2,1,0:T(8,128)} %copy-done, f32[32,17,8,128]{3,2,1,0:T(8,128)} %all_to_all.10.refs_1_), custom_call_target="tpu_custom_call" | custom-call | tf_op jit(solution)/shard_map/finish/pallas_call | solution.py:372
  134.4 3.0 %collective-permute-start.6 = (f32[1,256]{1,0:T(1,128)}, f32[1,256]{1,0:T(1,128)S(1)}, u32[]{:S(2)}, u32[]{:S(2)}) collective-permute-start(f32[1,256]{1,0:T(1,128)} %get-tuple-element.22), channel_id=1, source_target_pairs={{0,96},{32,0},{64,32},{96,64},{1,97},{33,1},{65,33},{97,65},{2,98}... | collective-permute-start | bytes 3080 | tf_op jit(solution)/shard_map/ppermute | solution.py:426
  137.4 0.6 collective-permute-start.5
  138.1 1.0 collective-permute-start.4
  139.0 1.4 reshape.36
  140.4 2.3 %collective-permute-done.5 = f32[1,256]{1,0:T(1,128)S(1)} collective-permute-done((f32[1,256]{1,0:T(1,128)}, f32[1,256]{1,0:T(1,128)S(1)}, u32[]{:S(2)}, u32[]{:S(2)}) %collective-permute-start.5) | collective-permute-done | bytes 1056 | tf_op jit(solution)/shard_map/ppermute | solution.py:426
  142.7 0.3 collective-permute-done.4
  143.1 1.2 add_multiply_fusion
  (7 shorter events, 0.0 us)
Async XLA Ops:
  6.1 65.6 %collective-permute-start.2 = (f32[8,1024,128]{2,1,0:T(8,128)}, f32[8,1024,128]{2,1,0:T(8,128)}, u32[]{:S(2)}, u32[]{:S(2)}) collective-permute-start(f32[8,1024,128]{2,1,0:T(8,128)} %get-tuple-element.16), channel_id=1, source_target_pairs={{0,1},{1,0},{2,3},{3,2},{4,5},{5,4},{6,7},{7,6},{8,9},{9,8},{10,11... | collective-permute-start | bytes 12582920 | tf_op jit(solution)/shard_map/ppermute | solution.py:402
  9.1 39.9 %collective-permute-start = (f32[4,1024,128]{2,1,0:T(8,128)}, f32[4,1024,128]{2,1,0:T(8,128)}, u32[]{:S(2)}, u32[]{:S(2)}) collective-permute-start(f32[4,1024,128]{2,1,0:T(8,128)} %get-tuple-element.13), channel_id=1, source_target_pairs={{0,1},{1,0},{2,3},{3,2},{4,5},{5,4},{6,7},{7,6},{8,9},{9,8},{10,11... | collective-permute-start | bytes 6291464 | tf_op jit(solution)/shard_map/ppermute | solution.py:402
  9.6 62.0 %collective-permute-start.3 = (f32[8,512,128]{2,1,0:T(8,128)}, f32[8,512,128]{2,1,0:T(8,128)S(1)}, u32[]{:S(2)}, u32[]{:S(2)}) collective-permute-start(f32[8,512,128]{2,1,0:T(8,128)} %get-tuple-element.17), channel_id=1, source_target_pairs={{2,0},{4,2},{6,4},{8,6},{10,8},{12,10},{14,12},{16,14},{18,16},{20... | collective-permute-start | bytes 6291464 | tf_op jit(solution)/shard_map/ppermute | solution.py:401
  10.9 38.1 %collective-permute-start.1 = (f32[4,512,128]{2,1,0:T(8,128)}, f32[4,512,128]{2,1,0:T(8,128)S(1)}, u32[]{:S(2)}, u32[]{:S(2)}) collective-permute-start(f32[4,512,128]{2,1,0:T(8,128)} %get-tuple-element.14), channel_id=1, source_target_pairs={{2,0},{4,2},{6,4},{8,6},{10,8},{12,10},{14,12},{16,14},{18,16},{20... | collective-permute-start | bytes 3145736 | tf_op jit(solution)/shard_map/ppermute | solution.py:401
  49.0 1.0 copy-start.2
  61.7 31.7 %all-to-all-start = ((f32[32,8,8,128]{3,2,1,0:T(8,128)}), f32[32,8,8,128]{3,2,1,0:T(8,128)S(1)}, u32[]{:S(2)}, u32[]{:S(2)}) async-start(f32[32,8,8,128]{3,2,1,0:T(8,128)} %get-tuple-element.15), calls=%async_computation | async-start | bytes 2097152 | tf_op jit(solution)/shard_map/all_to_all | solution.py:420
  71.6 1.4 copy-start.1
  93.3 37.8 %copy-start = (f32[32,8,8,128]{3,2,1,0:T(8,128)}, f32[32,8,8,128]{3,2,1,0:T(8,128)S(1)}, u32[]{:S(2)}) copy-start(f32[32,8,8,128]{3,2,1,0:T(8,128)S(1)} %all-to-all-done.refs_0_) | copy-start | bytes 3145732
  134.4 6.0 %collective-permute-start.6 = (f32[1,256]{1,0:T(1,128)}, f32[1,256]{1,0:T(1,128)S(1)}, u32[]{:S(2)}, u32[]{:S(2)}) collective-permute-start(f32[1,256]{1,0:T(1,128)} %get-tuple-element.22), channel_id=1, source_target_pairs={{0,96},{32,0},{64,32},{96,64},{1,97},{33,1},{65,33},{97,65},{2,98}... | collective-permute-start | bytes 3080 | tf_op jit(solution)/shard_map/ppermute | solution.py:426
  137.4 5.3 %collective-permute-start.5 = (f32[1,256]{1,0:T(1,128)}, f32[1,256]{1,0:T(1,128)S(1)}, u32[]{:S(2)}, u32[]{:S(2)}) collective-permute-start(f32[1,256]{1,0:T(1,128)} %get-tuple-element.22), channel_id=1, source_target_pairs={{0,64},{32,96},{64,0},{96,32},{1,65},{33,97},{65,1},{97,33},{2,66}... | collective-permute-start | bytes 3080 | tf_op jit(solution)/shard_map/ppermute | solution.py:426
  138.1 5.0 %collective-permute-start.4 = (f32[1,256]{1,0:T(1,128)}, f32[1,256]{1,0:T(1,128)S(1)}, u32[]{:S(2)}, u32[]{:S(2)}) collective-permute-start(f32[1,256]{1,0:T(1,128)} %get-tuple-element.22), channel_id=1, source_target_pairs={{0,32},{32,64},{64,96},{96,0},{1,33},{33,65},{65,97},{97,1},{2,34}... | collective-permute-start | bytes 3080 | tf_op jit(solution)/shard_map/ppermute | solution.py:426

commit v4 on v3

--- a/solution.py
+++ b/solution.py
@@ -14,7 +14,7 @@
 HALF = ROOT // 2
 TILE = 8
 LANES = 128
-CHUNKS = (4, 8)
+CHUNKS = (5, 7)
 STEPS = len(CHUNKS)
 SIDE = 12
 PLACES = 32
@@ -80,9 +80,9 @@
     step = pl.program_id(0)
     me = lax.axis_index("tm")
     core = me & 1
-    right = 1 - core
+    right = core
     near = pl.multiple_of(HALF + ROOT * core, HALF)
-    far = pl.multiple_of(HALF + ROOT * right, HALF)
+    far = pl.multiple_of(HALF + ROOT * (1 - core), HALF)
     outer_at = pl.multiple_of(right * (5 * HALF), HALF)
     outer_start = pl.multiple_of(right * (4 * HALF), HALF)
     starts = (HALF, 2 * HALF, 3 * HALF, outer_start)
@@ -90,17 +90,25 @@
     keep = jnp.where(inside, 1.0, 0.0).astype(jnp.float32)
     base = step
 
+    def load(u):
+        for c in range(TILE):
+            for src, at, size in (
+                (x_hbm.at[core * SIDE + first + u, :, c, 0, :], near, ROOT),
+                (remote_hbm.at[skip + u, :, c, 0, :], far, ROOT),
+                (halo_hbm.at[skip + u, :, c, 0, :], outer_at, HALF),
+            ):
+                pltpu.make_async_copy(src, x_buf.at[u, c, pl.ds(at, size), :], sems.at[u]).start()
+
     @pl.when(step == 0)
     def _():
-        for u in range(tiles):
-            for c in range(TILE):
-                for src, at, size in (
-                    (x_hbm.at[core * SIDE + first + u, :, c, 0, :], near, ROOT),
-                    (remote_hbm.at[skip + u, :, c, 0, :], far, ROOT),
-                    (halo_hbm.at[skip + u, :, c, 0, :], outer_at, HALF),
-                ):
-                    pltpu.make_async_copy(src, x_buf.at[u, c, pl.ds(at, size), :], sems.at[u]).start()
+        load(0)
+        if tiles > 1:
+            load(1)
         edges_ref[...] = edges_in_ref[...] if first else jnp.zeros((TILE, LANES), jnp.float32)
+
+    @pl.when(step + 2 < tiles)
+    def _():
+        load(step + 2)
 
     def wait_for(u):
         whole = x_buf.at[base + u, :, pl.ds(0, 5 * HALF), :]
@@ -277,13 +285,12 @@
 
 def gather_kernel(tiles, first, x_hbm, halo_out, swap_out, halo_buf, swap_buf, sems):
     core = lax.axis_index("tm") & 1
-    mine = core * SIDE + first
     theirs = (1 - core) * SIDE + first
     edge = pl.multiple_of(core * (HALF * TILE), HALF * TILE)
     loads = []
     stores = []
     for u in range(tiles):
-        source = x_hbm.at[mine + u, pl.ds(edge, HALF * TILE), :]
+        source = x_hbm.at[theirs + u, pl.ds(edge, HALF * TILE), :]
         loads.append(pltpu.make_async_copy(source, halo_buf.at[u], sems.at[0, u]))
         stores.append(pltpu.make_async_copy(halo_buf.at[u], halo_out.at[u], sems.at[1, u]))
     for u in range(tiles):
@@ -392,13 +399,13 @@
     row_tiles = rows // TILE
     segments = width // (SEG // 2) * count - 1
     x = strain.reshape(row_tiles, TILE, ROOT, LANES).swapaxes(1, 2).reshape(row_tiles, ROOT * TILE, LANES)
-    same = [(i + 2, i) for i in range(0, count - 2, 2)] + [(i, i + 2) for i in range(1, count - 2, 2)]
+    cross = [(i, i + 1) for i in range(1, count - 2, 2)] + [(i + 1, i) for i in range(1, count - 2, 2)]
     swap = [(i, i ^ 1) for i in range(count)]
 
     moved = []
     for at, tiles in ((0, CHUNKS[0]), (CHUNKS[0], SIDE - CHUNKS[0])):
         edge, other = gather(tiles, at, x)
-        halo = lax.ppermute(edge, "tm", same)
+        halo = lax.ppermute(edge, "tm", cross)
         remote = lax.ppermute(other, "tm", swap)
         moved.append((remote, halo))
     constants = dft_constants()

time: 145 us -> 122 us (0.84)
  waiting for transfers between devices: 39.4 us -> 4.82 us
  starting transfers between devices: 17.8 us -> 34 us
  blocking collectives: 37.7 us -> 32.5 us
    ppermute x2, waiting for transfers between devices: 36.8 us -> 0.01 us  [per_device(): halo = lax.ppermute(edge, 'tm', cross)]
    all_to_all x1, starting transfers between devices: 9.98 us -> 26.1 us  [per_device(): parts.append(lax.all_to_all(out, 'tm', 0, 0, tiled=True))]
    all_to_all x1, blocking collectives: 37.7 us -> 32.5 us  [per_device(): parts.append(lax.all_to_all(out, 'tm', 0, 0, tiled=True))]
    all_to_all x1, waiting for transfers between devices: 0.01 us -> 2.14 us  [per_device(): parts.append(lax.all_to_all(out, 'tm', 0, 0, tiled=True))]
  transfers between devices with their start and end apart: 8 -> 8, of which waited for: 3 -> 3; matrix products, arithmetic and copies ran while one was open for 1% -> 2% of each run, Pallas kernels for 24% -> 31%
where the time goes in v4:
time: 122 us
  Pallas kernels  44.7 us (37%)
  starting transfers between devices  34 us (28%)
  blocking collectives  32.5 us (27%)
  waiting for transfers between devices  4.82 us (4%)
  local copies, waits for them, and re-layouts  3.98 us (3%)
  other arithmetic  1.25 us (1%)
    all_to_all x1, blocking collectives, per_device(): parts.append(lax.all_to_all(out, 'tm', 0, 0, tiled=True))  32.5 us
    pallas_call x2, Pallas kernels, spectrum(): pl.pallas_call(functools.partial(spectrum_kernel, tiles, first, skip, las...  32.3 us
    all_to_all x1, starting transfers between devices, per_device(): parts.append(lax.all_to_all(out, 'tm', 0, 0, tiled=True))  26.1 us
    pallas_call x2, Pallas kernels, gather(): pl.pallas_call(functools.partial(gather_kernel, tiles, first), in_specs=[...  9.09 us
    ppermute x3, starting transfers between devices, per_device(): lax.ppermute(band_sum, 'chan', [(i, (i + shift) % chans) for i in range(c...  4.62 us
    pallas_call x1, Pallas kernels, finish(): pl.pallas_call(finish_kernel, in_specs=[smem, vmem] + [vmem] * len(parts)...  3.35 us
    ppermute x3, waiting for transfers between devices, per_device(): lax.ppermute(band_sum, 'chan', [(i, (i + shift) % chans) for i in range(c...  2.66 us
    ppermute x2, starting transfers between devices, per_device(): halo = lax.ppermute(edge, 'tm', cross)  2.64 us
  transfers between devices with their start and end apart: 8, of which 3 were waited for; matrix products, arithmetic and copies ran while one was open for 2% of the time, Pallas kernels for 31%

profile of v4, /device:TPU:0, one launch (start us, length us, event | category | flops | bytes accessed | tf_op | source)
XLA Modules:
  0.0 121.9 jit_solution(10076095327556977309)
XLA Ops:
  0.6 4.1 %gather.2 = (f32[5,512,128]{2,1,0:T(8,128)}, f32[5,1024,128]{2,1,0:T(8,128)}) custom-call(f32[24,1024,128]{2,1,0:T(8,128)} %bitcast.12), custom_call_target="tpu_custom_call" | custom-call | tf_op jit(solution)/shard_map/gather/pallas_call | solution.py:310
  4.7 0.1 collective-permute-start
  4.8 5.0 %gather.3 = (f32[7,512,128]{2,1,0:T(8,128)}, f32[7,1024,128]{2,1,0:T(8,128)}) custom-call(f32[24,1024,128]{2,1,0:T(8,128)} %bitcast.13), custom_call_target="tpu_custom_call" | custom-call | tf_op jit(solution)/shard_map/gather/pallas_call | solution.py:310
  9.8 0.6 collective-permute-start.2
  10.4 0.7 collective-permute-start.1
  11.2 1.9 %collective-permute-start.3 = (f32[7,512,128]{2,1,0:T(8,128)}, f32[7,512,128]{2,1,0:T(8,128)}, u32[]{:S(2)}, u32[]{:S(2)}) collective-permute-start(f32[7,512,128]{2,1,0:T(8,128)} %get-tuple-element.17), channel_id=1, source_target_pairs={{1,2},{3,4},{5,6},{7,8},{9,10},{11,12},{13,14},{15,16},{17,18},{19... | collective-permute-start | bytes 5505032 | tf_op jit(solution)/shard_map/ppermute | solution.py:408
  13.1 0.0 collective-permute-done.1
  13.1 1.1 copy-done.2
  14.1 0.6 jit_solution_.3.edges_in_ref
  14.8 0.9 copy-done.1
  15.7 13.9 %spectrum.2 = (f32[32,10,8,128]{3,2,1,0:T(8,128)}, f32[8,128]{1,0:T(8,128)}) custom-call(f32[24,128,8,1,128]{4,3,2,1,0:T(1,128)} %bitcast.14, f32[5,128,8,1,128]{4,3,2,1,0:T(1,128)} %bitcast.16, f32[5,64,8,1,128]{4,3,2,1,0:T(1,128)} %bitcast.17, f32[328,128]{1,0:T(8,128)} %constant.15.clone.reals_ref, bf16[128,384]{1,0:T(8,128)(2,1)} %constant.16.clone.first_ref, ...), custom_call_target="tpu_custom_call" | custom-call | flops 671088640 | bytes 10485760 | tf_op jit(solution)/shard_map/spectrum/pallas_call | solution.py:244
  29.6 26.1 %all-to-all-start = ((f32[32,10,8,128]{3,2,1,0:T(8,128)}), f32[32,10,8,128]{3,2,1,0:T(8,128)S(1)}, u32[]{:S(2)}, u32[]{:S(2)}) async-start(f32[32,10,8,128]{3,2,1,0:T(8,128)} %get-tuple-element.15), calls=%async_computation | async-start | bytes 2621440 | tf_op jit(solution)/shard_map/all_to_all | solution.py:427
  55.7 0.0 collective-permute-done.2
  55.7 18.4 %spectrum.3 = (f32[32,15,8,128]{3,2,1,0:T(8,128)}, f32[8,128]{1,0:T(8,128)}) custom-call(f32[24,128,8,1,128]{4,3,2,1,0:T(1,128)} %bitcast.15, f32[7,128,8,1,128]{4,3,2,1,0:T(1,128)} %bitcast.9.remote_hbm, f32[7,64,8,1,128]{4,3,2,1,0:T(1,128)} %bitcast.10.halo_hbm, f32[328,128]{1,0:T(8,128)} %constant.15.clone.reals_ref, ...), custom_call_target="tpu_custom_call" | custom-call | flops 939524096 | bytes 14680064 | tf_op jit(solution)/shard_map/spectrum/pallas_call | solution.py:244
  74.1 2.1 %all-to-all-done.refs_0_ = f32[32,10,8,128]{3,2,1,0:T(8,128)S(1)} async-done(((f32[32,10,8,128]{3,2,1,0:T(8,128)}), f32[32,10,8,128]{3,2,1,0:T(8,128)S(1)}, u32[]{:S(2)}, u32[]{:S(2)}) %all-to-all-start) | async-done | bytes 1310752 | tf_op jit(solution)/shard_map/all_to_all | solution.py:427
  76.2 32.5 %all_to_all.10.refs_1_ = f32[32,15,8,128]{3,2,1,0:T(8,128)} all-to-all(f32[32,15,8,128]{3,2,1,0:T(8,128)} %get-tuple-element.19), channel_id=1, replica_groups=mesh['chan'=4,'tm'=32] {'tm'}, dimensions={0} | all-to-all | bytes 3932160 | tf_op jit(solution)/shard_map/all_to_all | solution.py:427
  108.7 3.4 %finish.1 = (f32[192,256]{1,0:T(8,128)}, f32[1,256]{1,0:T(1,128)}, f32[24,8]{1,0:T(8,128)}) custom-call(f32[1]{0:T(128)} %constant.6.clone.1.scale_ref, f32[2,256,128]{2,1,0:T(8,128)} %constant.19.clone.pick_ref, f32[32,10,8,128]{3,2,1,0:T(8,128)} %copy-done, f32[32,15,8,128]{3,2,1,0:T(8,128)} %all_to_all.10.refs_1_), custom_call_target="tpu_custom_call" | custom-call | tf_op jit(solution)/shard_map/finish/pallas_call | solution.py:379
  112.0 3.0 %collective-permute-start.6 = (f32[1,256]{1,0:T(1,128)}, f32[1,256]{1,0:T(1,128)S(1)}, u32[]{:S(2)}, u32[]{:S(2)}) collective-permute-start(f32[1,256]{1,0:T(1,128)} %get-tuple-element.22), channel_id=1, source_target_pairs={{0,96},{32,0},{64,32},{96,64},{1,97},{33,1},{65,33},{97,65},{2,98}... | collective-permute-start | bytes 3080 | tf_op jit(solution)/shard_map/ppermute | solution.py:433
  115.1 0.6 collective-permute-start.5
  115.7 1.0 collective-permute-start.4
  116.7 1.4 %reshape.36 = f32[192]{0:T(256)} reshape(f32[24,8]{1,0:T(8,128)} %get-tuple-element.21) | data formatting | bytes 1536 | tf_op jit(solution)/shard_map/reshape | solution.py:435
  118.0 2.3 %collective-permute-done.5 = f32[1,256]{1,0:T(1,128)S(1)} collective-permute-done((f32[1,256]{1,0:T(1,128)}, f32[1,256]{1,0:T(1,128)S(1)}, u32[]{:S(2)}, u32[]{:S(2)}) %collective-permute-start.5) | collective-permute-done | bytes 1056 | tf_op jit(solution)/shard_map/ppermute | solution.py:433
  120.3 0.3 collective-permute-done.4
  120.7 1.2 %add_multiply_fusion = f32[1,256]{1,0:T(1,128)} fusion(f32[1,256]{1,0:T(1,128)S(1)} %collective-permute-done.6, f32[1,256]{1,0:T(1,128)S(1)} %collective-permute-done.5, f32[1,256]{1,0:T(1,128)} %get-tuple-element.22, f32[1,256]{1,0:T(1,128)S(1)} %collective-permute-done.4), kind=kLoop, calls=%fused_computation | loop fusion | flops 1024 | bytes 5120 | tf_op jit(solution)/shard_map/div | solution.py:434
  (7 shorter events, 0.0 us)
Async XLA Ops:
  4.7 8.3 %collective-permute-start = (f32[5,1024,128]{2,1,0:T(8,128)}, f32[5,1024,128]{2,1,0:T(8,128)S(1)}, u32[]{:S(2)}, u32[]{:S(2)}) collective-permute-start(f32[5,1024,128]{2,1,0:T(8,128)} %get-tuple-element.13), channel_id=1, source_target_pairs={{0,1},{1,0},{2,3},{3,2},{4,5},{5,4},{6,7},{7,6},{8,9},{9,8},{10,11... | collective-permute-start | bytes 7864328 | tf_op jit(solution)/shard_map/ppermute | solution.py:409
  9.8 45.9 %collective-permute-start.2 = (f32[7,1024,128]{2,1,0:T(8,128)}, f32[7,1024,128]{2,1,0:T(8,128)}, u32[]{:S(2)}, u32[]{:S(2)}) collective-permute-start(f32[7,1024,128]{2,1,0:T(8,128)} %get-tuple-element.16), channel_id=1, source_target_pairs={{0,1},{1,0},{2,3},{3,2},{4,5},{5,4},{6,7},{7,6},{8,9},{9,8},{10,11... | collective-permute-start | bytes 11010056 | tf_op jit(solution)/shard_map/ppermute | solution.py:409
  10.4 2.7 %collective-permute-start.1 = (f32[5,512,128]{2,1,0:T(8,128)}, f32[5,512,128]{2,1,0:T(8,128)S(1)}, u32[]{:S(2)}, u32[]{:S(2)}) collective-permute-start(f32[5,512,128]{2,1,0:T(8,128)} %get-tuple-element.14), channel_id=1, source_target_pairs={{1,2},{3,4},{5,6},{7,8},{9,10},{11,12},{13,14},{15,16},{17,18},{19... | collective-permute-start | bytes 3932168 | tf_op jit(solution)/shard_map/ppermute | solution.py:408
  11.2 44.5 %collective-permute-start.3 = (f32[7,512,128]{2,1,0:T(8,128)}, f32[7,512,128]{2,1,0:T(8,128)}, u32[]{:S(2)}, u32[]{:S(2)}) collective-permute-start(f32[7,512,128]{2,1,0:T(8,128)} %get-tuple-element.17), channel_id=1, source_target_pairs={{1,2},{3,4},{5,6},{7,8},{9,10},{11,12},{13,14},{15,16},{17,18},{19... | collective-permute-start | bytes 5505032 | tf_op jit(solution)/shard_map/ppermute | solution.py:408
  13.1 1.1 copy-start.2
  14.1 1.5 %copy-start.1 = (f32[5,1024,128]{2,1,0:T(8,128)}, f32[5,1024,128]{2,1,0:T(8,128)S(1)}, u32[]{:S(2)}) copy-start(f32[5,1024,128]{2,1,0:T(8,128)S(1)} %collective-permute-done) | copy-start | bytes 7864324
  29.6 46.6 %all-to-all-start = ((f32[32,10,8,128]{3,2,1,0:T(8,128)}), f32[32,10,8,128]{3,2,1,0:T(8,128)S(1)}, u32[]{:S(2)}, u32[]{:S(2)}) async-start(f32[32,10,8,128]{3,2,1,0:T(8,128)} %get-tuple-element.15), calls=%async_computation | async-start | bytes 2621440 | tf_op jit(solution)/shard_map/all_to_all | solution.py:427
  76.2 32.5 %copy-start = (f32[32,10,8,128]{3,2,1,0:T(8,128)}, f32[32,10,8,128]{3,2,1,0:T(8,128)S(1)}, u32[]{:S(2)}) copy-start(f32[32,10,8,128]{3,2,1,0:T(8,128)S(1)} %all-to-all-done.refs_0_) | copy-start | bytes 3932164
  112.0 6.0 %collective-permute-start.6 = (f32[1,256]{1,0:T(1,128)}, f32[1,256]{1,0:T(1,128)S(1)}, u32[]{:S(2)}, u32[]{:S(2)}) collective-permute-start(f32[1,256]{1,0:T(1,128)} %get-tuple-element.22), channel_id=1, source_target_pairs={{0,96},{32,0},{64,32},{96,64},{1,97},{33,1},{65,33},{97,65},{2,98}... | collective-permute-start | bytes 3080 | tf_op jit(solution)/shard_map/ppermute | solution.py:433
  115.1 5.3 %collective-permute-start.5 = (f32[1,256]{1,0:T(1,128)}, f32[1,256]{1,0:T(1,128)S(1)}, u32[]{:S(2)}, u32[]{:S(2)}) collective-permute-start(f32[1,256]{1,0:T(1,128)} %get-tuple-element.22), channel_id=1, source_target_pairs={{0,64},{32,96},{64,0},{96,32},{1,65},{33,97},{65,1},{97,33},{2,66}... | collective-permute-start | bytes 3080 | tf_op jit(solution)/shard_map/ppermute | solution.py:433
  115.7 5.0 %collective-permute-start.4 = (f32[1,256]{1,0:T(1,128)}, f32[1,256]{1,0:T(1,128)S(1)}, u32[]{:S(2)}, u32[]{:S(2)}) collective-permute-start(f32[1,256]{1,0:T(1,128)} %get-tuple-element.22), channel_id=1, source_target_pairs={{0,32},{32,64},{64,96},{96,0},{1,33},{33,65},{65,97},{97,1},{2,34}... | collective-permute-start | bytes 3080 | tf_op jit(solution)/shard_map/ppermute | solution.py:433

commit v5 on v4

--- a/solution.py
+++ b/solution.py
@@ -283,19 +283,18 @@
     )
 
 
-def gather_kernel(tiles, first, x_hbm, halo_out, swap_out, halo_buf, swap_buf, sems):
+def gather_kernel(tiles, first, kinds, x_hbm, *refs):
+    outs, buffers, sems = refs[: len(kinds)], refs[len(kinds) : -1], refs[-1]
     core = lax.axis_index("tm") & 1
     theirs = (1 - core) * SIDE + first
     edge = pl.multiple_of(core * (HALF * TILE), HALF * TILE)
     loads = []
     stores = []
-    for u in range(tiles):
-        source = x_hbm.at[theirs + u, pl.ds(edge, HALF * TILE), :]
-        loads.append(pltpu.make_async_copy(source, halo_buf.at[u], sems.at[0, u]))
-        stores.append(pltpu.make_async_copy(halo_buf.at[u], halo_out.at[u], sems.at[1, u]))
-    for u in range(tiles):
-        loads.append(pltpu.make_async_copy(x_hbm.at[theirs + u], swap_buf.at[u], sems.at[0, tiles + u]))
-        stores.append(pltpu.make_async_copy(swap_buf.at[u], swap_out.at[u], sems.at[1, tiles + u]))
+    for n, kind in enumerate(kinds):
+        for u in range(tiles):
+            source = x_hbm.at[theirs + u] if kind else x_hbm.at[theirs + u, pl.ds(edge, HALF * TILE), :]
+            loads.append(pltpu.make_async_copy(source, buffers[n].at[u], sems.at[0, n * tiles + u]))
+            stores.append(pltpu.make_async_copy(buffers[n].at[u], outs[n].at[u], sems.at[1, n * tiles + u]))
     for copy in loads:
         copy.start()
     for load, store in zip(loads, stores):
@@ -305,23 +304,20 @@
         copy.wait()
 
 
-def gather(tiles, first, x):
+def gather(tiles, first, x, only=None):
     hbm = pl.BlockSpec(memory_space=pl.ANY)
-    return pl.pallas_call(
-        functools.partial(gather_kernel, tiles, first),
+    kinds = (0, 1) if only is None else (only,)
+    shapes = [(tiles, (ROOT if kind else HALF) * TILE, LANES) for kind in kinds]
+    out = pl.pallas_call(
+        functools.partial(gather_kernel, tiles, first, kinds),
         in_specs=[hbm],
-        out_specs=[hbm, hbm],
-        out_shape=[
-            jax.ShapeDtypeStruct((tiles, HALF * TILE, LANES), jnp.float32),
-            jax.ShapeDtypeStruct((tiles, ROOT * TILE, LANES), jnp.float32),
-        ],
-        scratch_shapes=[
-            pltpu.VMEM((tiles, HALF * TILE, LANES), jnp.float32),
-            pltpu.VMEM((tiles, ROOT * TILE, LANES), jnp.float32),
-            pltpu.SemaphoreType.DMA((2, 2 * tiles)),
-        ],
+        out_specs=[hbm] * len(kinds),
+        out_shape=[jax.ShapeDtypeStruct(shape, jnp.float32) for shape in shapes],
+        scratch_shapes=[pltpu.VMEM(shape, jnp.float32) for shape in shapes]
+        + [pltpu.SemaphoreType.DMA((2, len(kinds) * tiles))],
         name="gather",
     )(x)
+    return out if only is None else out[0]
 
 
 def pick_constant():
@@ -403,14 +399,16 @@
     swap = [(i, i ^ 1) for i in range(count)]
 
     moved = []
-    for at, tiles in ((0, CHUNKS[0]), (CHUNKS[0], SIDE - CHUNKS[0])):
-        edge, other = gather(tiles, at, x)
+    for group, (at, tiles) in enumerate(((0, CHUNKS[0]), (CHUNKS[0], SIDE - CHUNKS[0]))):
+        edge, other = gather(tiles, at, x) if group else (gather(tiles, at, x, 0), None)
         halo = lax.ppermute(edge, "tm", cross)
+        if group == 0:
+            other = gather(tiles, at, x, 1)
         remote = lax.ppermute(other, "tm", swap)
         moved.append((remote, halo))
     constants = dft_constants()
     scale = jnp.full((1,), 1.0 / (segments * constants[3]), jnp.float32)
-    edges = np.zeros((TILE, LANES), np.float32)
+    edges = constants[0]
     parts = []
     done = 0
     for step, tiles in enumerate(CHUNKS):

time: 122 us -> 123 us (level)
    pallas_call x2 -> x3, Pallas kernels: 9.09 us -> 9.78 us  [gather(): pl.pallas_call(functools.partial(gather_kernel, tiles, first, kinds), in_...]
  transfers between devices with their start and end apart: 8 -> 8, of which waited for: 3 -> 3; matrix products, arithmetic and copies ran while one was open for 2% -> 1% of each run, Pallas kernels for 31% -> 32%
where the time goes in v5:
time: 123 us
  Pallas kernels  45.4 us (37%)
  starting transfers between devices  34 us (28%)
  blocking collectives  32.5 us (26%)
  waiting for transfers between devices  4.8 us (4%)
  local copies, waits for them, and re-layouts  3.99 us (3%)
  other arithmetic  1.25 us (1%)
    all_to_all x1, blocking collectives, per_device(): parts.append(lax.all_to_all(out, 'tm', 0, 0, tiled=True))  32.5 us
    pallas_call x2, Pallas kernels, spectrum(): pl.pallas_call(functools.partial(spectrum_kernel, tiles, first, skip, las...  32.3 us
    all_to_all x1, starting transfers between devices, per_device(): parts.append(lax.all_to_all(out, 'tm', 0, 0, tiled=True))  26.1 us
    pallas_call x3, Pallas kernels, gather(): pl.pallas_call(functools.partial(gather_kernel, tiles, first, kinds), in_...  9.78 us
    ppermute x3, starting transfers between devices, per_device(): lax.ppermute(band_sum, 'chan', [(i, (i + shift) % chans) for i in range(c...  4.62 us
    pallas_call x1, Pallas kernels, finish(): pl.pallas_call(finish_kernel, in_specs=[smem, vmem] + [vmem] * len(parts)...  3.35 us
    ppermute x3, waiting for transfers between devices, per_device(): lax.ppermute(band_sum, 'chan', [(i, (i + shift) % chans) for i in range(c...  2.66 us
    ppermute x2, starting transfers between devices, per_device(): halo = lax.ppermute(edge, 'tm', cross)  2.64 us
  transfers between devices with their start and end apart: 8, of which 3 were waited for; matrix products, arithmetic and copies ran while one was open for 1% of the time, Pallas kernels for 32%

profile of v5, /device:TPU:0, one launch (start us, length us, event | category | flops | bytes accessed | tf_op | source)
XLA Modules:
  0.0 122.6 jit_solution(17275780744362045550)
XLA Ops:
  0.6 2.7 %gather.3 = f32[5,1024,128]{2,1,0:T(8,128)} custom-call(f32[24,1024,128]{2,1,0:T(8,128)} %bitcast.12), custom_call_target="tpu_custom_call" | custom-call | tf_op jit(solution)/shard_map/gather/pallas_call | solution.py:311
  3.3 0.1 collective-permute-start
  3.4 5.0 %gather.5 = (f32[7,512,128]{2,1,0:T(8,128)}, f32[7,1024,128]{2,1,0:T(8,128)}) custom-call(f32[24,1024,128]{2,1,0:T(8,128)} %bitcast.13), custom_call_target="tpu_custom_call" | custom-call | tf_op jit(solution)/shard_map/gather/pallas_call | solution.py:311
  8.4 0.6 collective-permute-start.2
  9.0 2.1 %gather.4 = f32[5,512,128]{2,1,0:T(8,128)} custom-call(f32[24,1024,128]{2,1,0:T(8,128)} %bitcast.14), custom_call_target="tpu_custom_call" | custom-call | tf_op jit(solution)/shard_map/gather/pallas_call | solution.py:311
  11.1 0.7 collective-permute-start.1
  11.9 1.9 %collective-permute-start.3 = (f32[7,512,128]{2,1,0:T(8,128)}, f32[7,512,128]{2,1,0:T(8,128)}, u32[]{:S(2)}, u32[]{:S(2)}) collective-permute-start(f32[7,512,128]{2,1,0:T(8,128)} %get-tuple-element.13), channel_id=1, source_target_pairs={{1,2},{3,4},{5,6},{7,8},{9,10},{11,12},{13,14},{15,16},{17,18},{19... | collective-permute-start | bytes 5505032 | tf_op jit(solution)/shard_map/ppermute | solution.py:404
  13.8 0.0 collective-permute-done.1
  13.8 0.0 collective-permute-done
  13.8 1.1 copy-done.2
  14.8 1.5 %copy-done.1 = f32[5,1024,128]{2,1,0:T(8,128)} copy-done((f32[5,1024,128]{2,1,0:T(8,128)}, f32[5,1024,128]{2,1,0:T(8,128)S(1)}, u32[]{:S(2)}) %copy-start.1) | copy-done | bytes 2621464
  16.4 13.9 %spectrum.2 = (f32[32,10,8,128]{3,2,1,0:T(8,128)}, f32[8,128]{1,0:T(8,128)}) custom-call(f32[24,128,8,1,128]{4,3,2,1,0:T(1,128)} %bitcast.15, f32[5,128,8,1,128]{4,3,2,1,0:T(1,128)} %bitcast.17, f32[5,64,8,1,128]{4,3,2,1,0:T(1,128)} %bitcast.18, f32[328,128]{1,0:T(8,128)} %constant.13.clone.reals_ref.edges_in_ref, ...), custom_call_target="tpu_custom_call" | custom-call | flops 671088640 | bytes 10485760 | tf_op jit(solution)/shard_map/spectrum/pallas_call | solution.py:244
  30.3 26.1 %all-to-all-start = ((f32[32,10,8,128]{3,2,1,0:T(8,128)}), f32[32,10,8,128]{3,2,1,0:T(8,128)S(1)}, u32[]{:S(2)}, u32[]{:S(2)}) async-start(f32[32,10,8,128]{3,2,1,0:T(8,128)} %get-tuple-element.11), calls=%async_computation | async-start | bytes 2621440 | tf_op jit(solution)/shard_map/all_to_all | solution.py:425
  56.4 18.4 %spectrum.3 = (f32[32,15,8,128]{3,2,1,0:T(8,128)}, f32[8,128]{1,0:T(8,128)}) custom-call(f32[24,128,8,1,128]{4,3,2,1,0:T(1,128)} %bitcast.16, f32[7,128,8,1,128]{4,3,2,1,0:T(1,128)} %bitcast.9.remote_hbm, f32[7,64,8,1,128]{4,3,2,1,0:T(1,128)} %bitcast.10.halo_hbm, f32[328,128]{1,0:T(8,128)} %constant.13.clone.reals_ref.edges_in_ref, ...), custom_call_target="tpu_custom_call" | custom-call | flops 939524096 | bytes 14680064 | tf_op jit(solution)/shard_map/spectrum/pallas_call | solution.py:244
  74.8 2.1 %all-to-all-done.refs_0_ = f32[32,10,8,128]{3,2,1,0:T(8,128)S(1)} async-done(((f32[32,10,8,128]{3,2,1,0:T(8,128)}), f32[32,10,8,128]{3,2,1,0:T(8,128)S(1)}, u32[]{:S(2)}, u32[]{:S(2)}) %all-to-all-start) | async-done | bytes 1310752 | tf_op jit(solution)/shard_map/all_to_all | solution.py:425
  76.9 32.5 %all_to_all.10.refs_1_ = f32[32,15,8,128]{3,2,1,0:T(8,128)} all-to-all(f32[32,15,8,128]{3,2,1,0:T(8,128)} %get-tuple-element.15), channel_id=1, replica_groups=mesh['chan'=4,'tm'=32] {'tm'}, dimensions={0} | all-to-all | bytes 3932160 | tf_op jit(solution)/shard_map/all_to_all | solution.py:425
  109.4 3.4 %finish.1 = (f32[192,256]{1,0:T(8,128)}, f32[1,256]{1,0:T(1,128)}, f32[24,8]{1,0:T(8,128)}) custom-call(f32[1]{0:T(128)} %constant.5.clone.1.scale_ref, f32[2,256,128]{2,1,0:T(8,128)} %constant.16.clone.pick_ref, f32[32,10,8,128]{3,2,1,0:T(8,128)} %copy-done, f32[32,15,8,128]{3,2,1,0:T(8,128)} %all_to_all.10.refs_1_), custom_call_target="tpu_custom_call" | custom-call | tf_op jit(solution)/shard_map/finish/pallas_call | solution.py:375
  112.8 3.0 %collective-permute-start.6 = (f32[1,256]{1,0:T(1,128)}, f32[1,256]{1,0:T(1,128)S(1)}, u32[]{:S(2)}, u32[]{:S(2)}) collective-permute-start(f32[1,256]{1,0:T(1,128)} %get-tuple-element.18), channel_id=1, source_target_pairs={{0,96},{32,0},{64,32},{96,64},{1,97},{33,1},{65,33},{97,65},{2,98}... | collective-permute-start | bytes 3080 | tf_op jit(solution)/shard_map/ppermute | solution.py:431
  115.8 0.6 collective-permute-start.5
  116.4 1.0 collective-permute-start.4
  117.4 1.4 %reshape.36 = f32[192]{0:T(256)} reshape(f32[24,8]{1,0:T(8,128)} %get-tuple-element.17) | data formatting | bytes 1536 | tf_op jit(solution)/shard_map/reshape | solution.py:433
  118.7 2.3 %collective-permute-done.5 = f32[1,256]{1,0:T(1,128)S(1)} collective-permute-done((f32[1,256]{1,0:T(1,128)}, f32[1,256]{1,0:T(1,128)S(1)}, u32[]{:S(2)}, u32[]{:S(2)}) %collective-permute-start.5) | collective-permute-done | bytes 1056 | tf_op jit(solution)/shard_map/ppermute | solution.py:431
  121.1 0.3 collective-permute-done.4
  121.4 1.2 %add_multiply_fusion = f32[1,256]{1,0:T(1,128)} fusion(f32[1,256]{1,0:T(1,128)S(1)} %collective-permute-done.6, f32[1,256]{1,0:T(1,128)S(1)} %collective-permute-done.5, f32[1,256]{1,0:T(1,128)} %get-tuple-element.18, f32[1,256]{1,0:T(1,128)S(1)} %collective-permute-done.4), kind=kLoop, calls=%fused_computation | loop fusion | flops 1024 | bytes 5120 | tf_op jit(solution)/shard_map/div | solution.py:432
  (7 shorter events, 0.0 us)
Async XLA Ops:
  3.3 10.4 %collective-permute-start = (f32[5,1024,128]{2,1,0:T(8,128)}, f32[5,1024,128]{2,1,0:T(8,128)S(1)}, u32[]{:S(2)}, u32[]{:S(2)}) collective-permute-start(f32[5,1024,128]{2,1,0:T(8,128)} %gather.3), channel_id=1, source_target_pairs={{0,1},{1,0},{2,3},{3,2},{4,5},{5,4},{6,7},{7,6},{8,9},{9,8},{10,11... | collective-permute-start | bytes 7864328 | tf_op jit(solution)/shard_map/ppermute | solution.py:407
  8.4 48.0 %collective-permute-start.2 = (f32[7,1024,128]{2,1,0:T(8,128)}, f32[7,1024,128]{2,1,0:T(8,128)}, u32[]{:S(2)}, u32[]{:S(2)}) collective-permute-start(f32[7,1024,128]{2,1,0:T(8,128)} %get-tuple-element.12), channel_id=1, source_target_pairs={{0,1},{1,0},{2,3},{3,2},{4,5},{5,4},{6,7},{7,6},{8,9},{9,8},{10,11... | collective-permute-start | bytes 11010056 | tf_op jit(solution)/shard_map/ppermute | solution.py:407
  11.1 2.7 %collective-permute-start.1 = (f32[5,512,128]{2,1,0:T(8,128)}, f32[5,512,128]{2,1,0:T(8,128)S(1)}, u32[]{:S(2)}, u32[]{:S(2)}) collective-permute-start(f32[5,512,128]{2,1,0:T(8,128)} %gather.4), channel_id=1, source_target_pairs={{1,2},{3,4},{5,6},{7,8},{9,10},{11,12},{13,14},{15,16},{17,18},{19... | collective-permute-start | bytes 3932168 | tf_op jit(solution)/shard_map/ppermute | solution.py:404
  11.9 44.5 %collective-permute-start.3 = (f32[7,512,128]{2,1,0:T(8,128)}, f32[7,512,128]{2,1,0:T(8,128)}, u32[]{:S(2)}, u32[]{:S(2)}) collective-permute-start(f32[7,512,128]{2,1,0:T(8,128)} %get-tuple-element.13), channel_id=1, source_target_pairs={{1,2},{3,4},{5,6},{7,8},{9,10},{11,12},{13,14},{15,16},{17,18},{19... | collective-permute-start | bytes 5505032 | tf_op jit(solution)/shard_map/ppermute | solution.py:404
  13.8 1.1 copy-start.2
  14.8 1.5 %copy-start.1 = (f32[5,1024,128]{2,1,0:T(8,128)}, f32[5,1024,128]{2,1,0:T(8,128)S(1)}, u32[]{:S(2)}) copy-start(f32[5,1024,128]{2,1,0:T(8,128)S(1)} %collective-permute-done) | copy-start | bytes 7864324
  30.3 46.6 %all-to-all-start = ((f32[32,10,8,128]{3,2,1,0:T(8,128)}), f32[32,10,8,128]{3,2,1,0:T(8,128)S(1)}, u32[]{:S(2)}, u32[]{:S(2)}) async-start(f32[32,10,8,128]{3,2,1,0:T(8,128)} %get-tuple-element.11), calls=%async_computation | async-start | bytes 2621440 | tf_op jit(solution)/shard_map/all_to_all | solution.py:425
  76.9 32.5 %copy-start = (f32[32,10,8,128]{3,2,1,0:T(8,128)}, f32[32,10,8,128]{3,2,1,0:T(8,128)S(1)}, u32[]{:S(2)}) copy-start(f32[32,10,8,128]{3,2,1,0:T(8,128)S(1)} %all-to-all-done.refs_0_) | copy-start | bytes 3932164
  112.8 6.0 %collective-permute-start.6 = (f32[1,256]{1,0:T(1,128)}, f32[1,256]{1,0:T(1,128)S(1)}, u32[]{:S(2)}, u32[]{:S(2)}) collective-permute-start(f32[1,256]{1,0:T(1,128)} %get-tuple-element.18), channel_id=1, source_target_pairs={{0,96},{32,0},{64,32},{96,64},{1,97},{33,1},{65,33},{97,65},{2,98}... | collective-permute-start | bytes 3080 | tf_op jit(solution)/shard_map/ppermute | solution.py:431
  115.8 5.3 %collective-permute-start.5 = (f32[1,256]{1,0:T(1,128)}, f32[1,256]{1,0:T(1,128)S(1)}, u32[]{:S(2)}, u32[]{:S(2)}) collective-permute-start(f32[1,256]{1,0:T(1,128)} %get-tuple-element.18), channel_id=1, source_target_pairs={{0,64},{32,96},{64,0},{96,32},{1,65},{33,97},{65,1},{97,33},{2,66}... | collective-permute-start | bytes 3080 | tf_op jit(solution)/shard_map/ppermute | solution.py:431
  116.4 5.0 %collective-permute-start.4 = (f32[1,256]{1,0:T(1,128)}, f32[1,256]{1,0:T(1,128)S(1)}, u32[]{:S(2)}, u32[]{:S(2)}) collective-permute-start(f32[1,256]{1,0:T(1,128)} %get-tuple-element.18), channel_id=1, source_target_pairs={{0,32},{32,64},{64,96},{96,0},{1,33},{33,65},{65,97},{97,1},{2,34}... | collective-permute-start | bytes 3080 | tf_op jit(solution)/shard_map/ppermute | solution.py:431
